TPU v7x, 128 devices: a whole 4x4x4 slice. The times are simulated.
128 devices in a mesh: dp: 1, sp: 128 (over z, y, x, core).
Axes of the slice: x: 4, y: 4, z: 4, core: 2. Of those that a mesh axis runs over, the one named last changes fastest.
Arguments:
- patches: bfloat16 [2, 8192, 768], P('dp', 'sp')
- vis_mask: int32 [2, 8192], P('dp', 'sp')
- enc_pos: bfloat16 [8192, 1024], P(('dp', 'sp'))
- dec_pos: bfloat16 [8192, 512], P(('dp', 'sp'))
- w_pe: bfloat16 [768, 1024], replicated
- b_pe: bfloat16 [1024], replicated
- enc_qkv: bfloat16 [2, 1024, 3, 16, 64], replicated
- enc_proj: bfloat16 [2, 16, 64, 1024], replicated
- enc_up: bfloat16 [2, 1024, 4096], replicated
- enc_down: bfloat16 [2, 4096, 1024], replicated
- w_ed: bfloat16 [1024, 512], replicated
- mask_token: bfloat16 [512], replicated
- dec_qkv: bfloat16 [2, 512, 3, 16, 32], replicated
- dec_proj: bfloat16 [2, 16, 32, 512], replicated
- dec_up: bfloat16 [2, 512, 2048], replicated
- dec_down: bfloat16 [2, 2048, 512], replicated
- w_out: bfloat16 [512, 768], replicated
Outputs:
- output: float32 [2, 8192, 768], P('dp', 'sp')
All inputs are finite; a program needn't handle non-finite values.
Results may differ from a plain program's by a relative error of at most 0.0153618.
Values are sent between devices in bfloat16 or wider.
A program may use at most 1 GiB of HBM per device.

v0:
```python
import jax
import jax.numpy as jnp
from jax import lax
from jax.sharding import PartitionSpec as P

KEEP_DIV = 8


def layer_norm(hidden):
    hid_f32 = hidden.astype(jnp.float32)
    centred = hid_f32 - jnp.mean(hid_f32, axis=-1, keepdims=True)
    row_var = jnp.mean(centred * centred, axis=-1, keepdims=True)
    return (centred * lax.rsqrt(row_var + 1e-6)).astype(jnp.bfloat16)


def attn_mlp_block(hidden, w_qkv, w_proj, w_up, w_down):
    proj_qkv = jnp.einsum('cnd,dshk->scnhk', layer_norm(hidden), w_qkv, preferred_element_type=jnp.float32).astype(jnp.bfloat16)
    kv_all = lax.all_gather(proj_qkv[1:], 'sp', axis=2, tiled=True)
    scores = jnp.einsum('cqhk,cshk->chqs', proj_qkv[0], kv_all[0], preferred_element_type=jnp.float32) * proj_qkv.shape[-1] ** -0.5
    attn_probs = jax.nn.softmax(scores, axis=-1).astype(jnp.bfloat16)
    attended = jnp.einsum('chqs,cshk->cqhk', attn_probs, kv_all[1], preferred_element_type=jnp.float32).astype(jnp.bfloat16)
    mid_state = (hidden + jnp.einsum('cqhk,hkd->cqd', attended, w_proj, preferred_element_type=jnp.float32)).astype(jnp.bfloat16)
    up_act = jax.nn.gelu(jnp.einsum('cnd,df->cnf', layer_norm(mid_state), w_up, preferred_element_type=jnp.float32), approximate=False).astype(jnp.bfloat16)
    return (mid_state + jnp.einsum('cnf,fd->cnd', up_act, w_down, preferred_element_type=jnp.float32)).astype(jnp.bfloat16)


def solution(mesh):
    group_size = mesh.shape['sp']
    to_next = [(src_dev, src_dev + 1) for src_dev in range(group_size - 1)]
    to_prev = [(src_dev + 1, src_dev) for src_dev in range(group_size - 1)]

    def local_program(patches, vis_mask, enc_pos, dec_pos, w_pe, b_pe, enc_qkv, enc_proj, enc_up, enc_down, w_ed, mask_token, dec_qkv, dec_proj, dec_up, dec_down, w_out):
        vis_shard = patches.shape[1] // KEEP_DIV
        half_rows = vis_shard // 2
        my_index = lax.axis_index('sp')
        vis_counts = lax.all_gather(jnp.sum(vis_mask, axis=1), 'sp')
        vis_before = jnp.sum(jnp.where(jnp.arange(group_size)[:, None] < my_index, vis_counts, 0), axis=0)
        local_rank = jnp.cumsum(vis_mask, axis=1) - vis_mask
        dest_row = vis_before[:, None] + local_rank - my_index * vis_shard + half_rows
        row_ids = jnp.arange(2 * vis_shard)
        select = ((dest_row[:, None, :] == row_ids[None, :, None]) & (vis_mask[:, None, :] == 1)).astype(jnp.bfloat16)
        moved_x = jnp.einsum('cqi,cip->cqp', select, patches, preferred_element_type=jnp.float32).astype(jnp.bfloat16)
        moved_pos = jnp.einsum('cqi,id->cqd', select, enc_pos, preferred_element_type=jnp.float32)
        occupied = jnp.sum(select, axis=2, dtype=jnp.float32)
        embedded = (jnp.einsum('cqp,pd->cqd', moved_x, w_pe, preferred_element_type=jnp.float32)
                    + occupied[:, :, None] * b_pe.astype(jnp.float32) + moved_pos).astype(jnp.bfloat16)
        from_prev = lax.ppermute(embedded[:, 3 * half_rows:], 'sp', to_next)
        from_next = lax.ppermute(embedded[:, :half_rows], 'sp', to_prev)
        hidden = embedded[:, half_rows:3 * half_rows] + jnp.concatenate([from_prev, from_next], axis=1)
        for layer_idx in range(enc_qkv.shape[0]):
            hidden = attn_mlp_block(hidden, enc_qkv[layer_idx], enc_proj[layer_idx], enc_up[layer_idx], enc_down[layer_idx])
        z_enc = jnp.einsum('cnd,de->cne', layer_norm(hidden), w_ed, preferred_element_type=jnp.float32).astype(jnp.bfloat16)
        z_prev = lax.ppermute(z_enc[:, half_rows:], 'sp', to_next)
        z_next = lax.ppermute(z_enc[:, :half_rows], 'sp', to_prev)
        z_rows = jnp.concatenate([z_prev, z_enc, z_next], axis=1)
        placed = jnp.einsum('cqi,cqe->cie', select, z_rows, preferred_element_type=jnp.float32)
        masked_part = (1 - vis_mask).astype(jnp.float32)[:, :, None] * mask_token.astype(jnp.float32)
        hidden = (placed + masked_part + dec_pos.astype(jnp.float32)).astype(jnp.bfloat16)
        for layer_idx in range(dec_qkv.shape[0]):
            hidden = attn_mlp_block(hidden, dec_qkv[layer_idx], dec_proj[layer_idx], dec_up[layer_idx], dec_down[layer_idx])
        return jnp.einsum('cne,ep->cnp', layer_norm(hidden), w_out, preferred_element_type=jnp.float32)

    row_spec = P('dp', 'sp', None)
    pos_spec = P(('dp', 'sp'), None)
    arg_specs = (row_spec, P('dp', 'sp'), pos_spec, pos_spec) + (P(),) * 13
    return jax.shard_map(local_program, mesh=mesh, in_specs=arg_specs, out_specs=row_spec, check_vma=False)
```

profile of v0, /device:TPU:1, one launch (start us, length us, event | category | flops | bytes accessed | tf_op | source)
XLA Modules:
  0.0 1645.6 jit_solution(4042048029775866891)
XLA Ops:
  9.3 68.7 %all-reduce = s32[256]{0:T(256)S(1)} all-reduce(s32[256]{0:T(256)S(1)} %dynamic-update-slice), channel_id=2, replica_groups=mesh['dp'=1,'sp'=128] {'sp'}, use_global_device_ids=true, to_apply=%add | all-reduce | flops 256 | bytes 2048
  82.2 2.6 collective-permute-start
  86.8 3.1 collective-permute-done.1
  90.2 5.4 fusion.146
  96.3 102.6 %all-gather.6.cloned.1.call-done = bf16[2,2,1024,16,64]{4,2,3,0,1:T(8,128)(2,1)} async-done(((bf16[2,2,8,16,64]{4,2,3,0,1:T(8,128)(2,1)}), bf16[2,2,1024,16,64]{4,2,3,0,1:T(8,128)(2,1)}) %all-gather.6.cloned.1.call-update) | async-done | bytes 8388624 | tf_op jit(solution)/shard_map/all_gather | solution.py:18
  198.9 5.8 fusion.573
  204.8 5.6 fusion.574
  210.6 4.8 fusion.403
  215.4 5.3 fusion.575
  224.5 99.0 %all-gather.8.cloned.1.call-done = bf16[2,2,1024,16,64]{4,2,3,0,1:T(8,128)(2,1)} async-done(((bf16[2,2,8,16,64]{4,2,3,0,1:T(8,128)(2,1)}), bf16[2,2,1024,16,64]{4,2,3,0,1:T(8,128)(2,1)}) %all-gather.8.cloned.1.call-update) | async-done | bytes 8388624 | tf_op jit(solution)/shard_map/all_gather | solution.py:18
  323.5 5.8 fusion.576
  329.3 5.6 fusion.577
  335.1 4.8 fusion.404
  340.0 5.1 fusion.578
  345.6 2.9 collective-permute-start.2
  350.6 3.0 collective-permute-done.3
  358.2 287.0 %all-gather.10.cloned.1.call-done = bf16[2,2,8192,16,32]{4,3,1,0,2:T(8,128)(2,1)} async-done(((bf16[2,2,64,16,32]{4,3,1,0,2:T(8,128)(2,1)}), bf16[2,2,8192,16,32]{4,3,1,0,2:T(8,128)(2,1)}) %all-gather.10.cloned.1.call-update) | async-done | bytes 33554448 | tf_op jit(solution)/shard_map/all_gather | solution.py:18
  645.2 88.6 %fusion.570 = (bf16[1,2,8192,16,32]{4,3,1,0,2:T(8,128)(2,1)}, bf16[1,2,8192,16,32]{4,3,1,0,2:T(8,128)(2,1)}) fusion(bf16[2,2,8192,16,32]{4,3,1,0,2:T(8,128)(2,1)} %all-gather.10.cloned.1.call-done), kind=kLoop, calls=%fused_computation.592 | loop fusion | bytes 67108864 | tf_op jit(solution)/shard_map/slice | solution.py:21
  733.8 66.3 %copy.44 = bf16[1,2,8192,16,32]{2,4,3,1,0:T(8,128)(2,1)} copy(bf16[1,2,8192,16,32]{4,3,1,0,2:T(8,128)(2,1)} %get-tuple-element.17) | data formatting | bytes 33554432
  800.1 66.3 %copy.45 = bf16[1,2,8192,16,32]{2,4,3,1,0:T(8,128)(2,1)} copy(bf16[1,2,8192,16,32]{4,3,1,0,2:T(8,128)(2,1)} %get-tuple-element.18) | data formatting | bytes 33554432
  866.4 28.6 %fusion.17 = f32[2,16,64,8192]{3,2,1,0:T(8,128)} fusion(bf16[1,2,8192,16,32]{2,4,3,1,0:T(8,128)(2,1)} %copy.45, bf16[3,2,64,16,32]{2,4,3,0,1:T(8,128)(2,1)S(1)} %fusion.83), kind=kOutput, calls=%fused_computation.19 | convolution fusion | flops 1073741824 | bytes 84148224 | tf_op jit(solution)/shard_map/cqhk,cshk->chqs/dot_general | solution.py:19
  894.9 68.7 %fusion.580 = (f32[2,16,64]{2,1,0:T(8,128)S(1)}, f32[2,16,64,8192]{3,2,1,0:T(8,128)}) fusion(f32[2,16,64,8192]{3,2,1,0:T(8,128)} %fusion.17), kind=kOutput, calls=%fused_computation.602 | output fusion | flops 67117056 | bytes 134225920 | tf_op jit(solution)/shard_map/sub | solution.py:20
  963.7 28.0 %fusion.581 = (f32[2,64]{1,0:T(2,128)S(1)}, f32[2,64,512]{2,1,0:T(8,128)S(1)}) fusion(f32[2,64,512]{2,1,0:T(8,128)S(1)} %copy-done.4, bf16[2,16,32,512]{3,2,1,0:T(8,128)(2,1)S(1)} %copy-done.12, f32[2,16,64,8192]{3,2,1,0:T(8,128)} %get-tuple-element.42, f32[2,16,64]{2,1,0:T(8,128)S(1)} %get-tuple-element.41, bf16[1,2,8192,16,32]{2,4,3,1,0:T(8,128)(2,1)} %copy.44), kind=kOutput, calls=%fused_computation.603 | convolution fusion | flops 1174732672 | bytes 84951552 | tf_op jit(solution)/shard_map/cqhk,hkd->cqd/dot_general | solution.py:22
  994.4 4.2 fusion.584
  1002.0 282.1 %all-gather.12.cloned.1.call-done = bf16[2,2,8192,16,32]{4,3,1,0,2:T(8,128)(2,1)} async-done(((bf16[2,2,64,16,32]{4,3,1,0,2:T(8,128)(2,1)}), bf16[2,2,8192,16,32]{4,3,1,0,2:T(8,128)(2,1)}) %all-gather.12.cloned.1.call-update) | async-done | bytes 33554448 | tf_op jit(solution)/shard_map/all_gather | solution.py:18
  1284.1 88.6 %fusion.569 = (bf16[1,2,8192,16,32]{4,3,1,0,2:T(8,128)(2,1)}, bf16[1,2,8192,16,32]{4,3,1,0,2:T(8,128)(2,1)}) fusion(bf16[2,2,8192,16,32]{4,3,1,0,2:T(8,128)(2,1)} %all-gather.12.cloned.1.call-done), kind=kLoop, calls=%fused_computation.591 | loop fusion | bytes 67108864 | tf_op jit(solution)/shard_map/slice | solution.py:21
  1372.7 66.3 %copy.46 = bf16[1,2,8192,16,32]{2,4,3,1,0:T(8,128)(2,1)} copy(bf16[1,2,8192,16,32]{4,3,1,0,2:T(8,128)(2,1)} %get-tuple-element.15) | data formatting | bytes 33554432
  1439.0 66.3 %copy.47 = bf16[1,2,8192,16,32]{2,4,3,1,0:T(8,128)(2,1)} copy(bf16[1,2,8192,16,32]{4,3,1,0,2:T(8,128)(2,1)} %get-tuple-element.16) | data formatting | bytes 33554432
  1505.3 28.6 %fusion.14 = f32[2,16,64,8192]{3,2,1,0:T(8,128)} fusion(bf16[1,2,8192,16,32]{2,4,3,1,0:T(8,128)(2,1)} %copy.47, bf16[3,2,64,16,32]{2,4,3,0,1:T(8,128)(2,1)S(1)} %fusion.80), kind=kOutput, calls=%fused_computation.16 | convolution fusion | flops 1073741824 | bytes 84148224 | tf_op jit(solution)/shard_map/cqhk,cshk->chqs/dot_general | solution.py:19
  1533.9 68.7 %fusion.585 = (f32[2,16,64]{2,1,0:T(8,128)S(1)}, f32[2,16,64,8192]{3,2,1,0:T(8,128)}) fusion(f32[2,16,64,8192]{3,2,1,0:T(8,128)} %fusion.14), kind=kOutput, calls=%fused_computation.605 | output fusion | flops 67117056 | bytes 134225920 | tf_op jit(solution)/shard_map/sub | solution.py:20
  1602.6 28.2 %fusion.586 = (f32[2,64]{1,0:T(2,128)S(1)}, f32[2,64,512]{2,1,0:T(8,128)S(1)}) fusion(f32[2,64,512]{2,1,0:T(8,128)S(1)} %copy-done.7, bf16[2,16,32,512]{3,2,1,0:T(8,128)(2,1)S(1)} %copy-done.13, f32[2,16,64,8192]{3,2,1,0:T(8,128)} %get-tuple-element.49, f32[2,16,64]{2,1,0:T(8,128)S(1)} %get-tuple-element.48, bf16[1,2,8192,16,32]{2,4,3,1,0:T(8,128)(2,1)} %copy.46), kind=kOutput, calls=%fused_computation.606 | convolution fusion | flops 1174732672 | bytes 84951552 | tf_op jit(solution)/shard_map/cqhk,hkd->cqd/dot_general | solution.py:22
  1633.5 4.0 fusion.589
  (109 shorter events, 31.0 us)
Async XLA Ops:
  6.5 73.2 %copy-start = (bf16[768,1024]{1,0:T(8,128)(2,1)S(1)}, bf16[768,1024]{1,0:T(8,128)(2,1)}, u32[]{:S(2)}) copy-start(bf16[768,1024]{1,0:T(8,128)(2,1)} %param.21) | copy-start | bytes 4718596
  6.5 192.4 %all-gather.6.cloned.1.call-start = ((), (), s32[]{:S(2)}) async-start(), calls=%async_computation | async-start | bytes 16908288 | tf_op jit(solution)/shard_map/all_gather | solution.py:18
  82.2 4.5 collective-permute-start
  84.8 5.1 collective-permute-start.1
  96.3 227.2 %all-gather.8.cloned.1.call-start = ((), (), s32[]{:S(2)}) async-start(), calls=%async_computation.1 | async-start | bytes 16908288 | tf_op jit(solution)/shard_map/all_gather | solution.py:18
  210.4 10.5 slice-start
  210.6 10.3 slice-start.1
  215.4 5.5 slice-start.2
  224.2 421.0 %all-gather.10.cloned.1.call-start = ((), (), s32[]{:S(2)}) async-start(), calls=%async_computation.2 | async-start | bytes 135266304 | tf_op jit(solution)/shard_map/all_gather | solution.py:18
  334.9 10.4 copy-start.2
  334.9 15.6 copy-start.9
  334.9 15.6 copy-start.8
  334.9 19.6 %copy-start.10 = (bf16[2,512,3,16,32]{1,4,3,2,0:T(8,128)(2,1)S(1)}, bf16[2,512,3,16,32]{1,4,3,2,0:T(8,128)(2,1)}, u32[]{:S(2)}) copy-start(bf16[2,512,3,16,32]{1,4,3,2,0:T(8,128)(2,1)} %param.29) | copy-start | bytes 9437188
  345.6 4.9 collective-permute-start.2
  348.6 5.0 collective-permute-start.3
  353.8 0.7 copy-start.3
  357.7 926.3 %all-gather.12.cloned.1.call-start = ((), (), s32[]{:S(2)}) async-start(), calls=%async_computation.3 | async-start | bytes 135266304 | tf_op jit(solution)/shard_map/all_gather | solution.py:18
  894.9 68.8 %copy-start.4 = (f32[2,64,512]{2,1,0:T(8,128)S(1)}, f32[2,64,512]{2,1,0:T(8,128)}, u32[]{:S(2)}) copy-start(f32[2,64,512]{2,1,0:T(8,128)} %copy-done.3) | copy-start | bytes 786436
  894.9 68.8 %copy-start.12 = (bf16[2,16,32,512]{3,2,1,0:T(8,128)(2,1)S(1)}, bf16[2,16,32,512]{3,2,1,0:T(8,128)(2,1)}, u32[]{:S(2)}) copy-start(bf16[2,16,32,512]{3,2,1,0:T(8,128)(2,1)} %param.30) | copy-start | bytes 3145732
  991.9 6.9 copy-start.11
  998.6 374.1 %copy-start.6 = (f32[2,64,512]{2,1,0:T(8,128)}, f32[2,64,512]{2,1,0:T(8,128)S(1)}, u32[]{:S(2)}) copy-start(f32[2,64,512]{2,1,0:T(8,128)S(1)} %get-tuple-element.47) | copy-start | bytes 786436
  1533.8 68.8 %copy-start.7 = (f32[2,64,512]{2,1,0:T(8,128)S(1)}, f32[2,64,512]{2,1,0:T(8,128)}, u32[]{:S(2)}) copy-start(f32[2,64,512]{2,1,0:T(8,128)} %copy-done.6) | copy-start | bytes 786436
  1533.8 68.8 %copy-start.13 = (bf16[2,16,32,512]{3,2,1,0:T(8,128)(2,1)S(1)}, bf16[2,16,32,512]{3,2,1,0:T(8,128)(2,1)}, u32[]{:S(2)}) copy-start(bf16[2,16,32,512]{3,2,1,0:T(8,128)(2,1)} %param.30) | copy-start | bytes 3145732
  1631.0 7.8 copy-start.1
  1631.0 6.7 copy-start.5
Sparse Core Ops, SparseCore 0:
  96.4 102.5 all-gather.5
  224.3 99.1 all-gather.7
  357.8 287.2 all-gather.9
  1002.1 281.8 all-gather.11
where the time goes:
time: 1660 us; the launch traced here: 1650 us
  waiting for transfers between devices  777 us (47%)
  local copies, waits for them, and re-layouts  450 us (27%)
  matrix products  183 us (11%)
  other arithmetic  144 us (9%)
  blocking collectives  68.7 us (4%)
    all_gather x4, waiting for transfers between devices, attn_mlp_block(): kv_all = lax.all_gather(proj_qkv[1:], 'sp', axis=2, tiled=True)  771 us
    unnamed x40, local copies, waits for them, and re-layouts  266 us
    slice x2, local copies, waits for them, and re-layouts, attn_mlp_block(): kv_all[1]  177 us
    sub x2, other arithmetic, attn_mlp_block(): attn_probs = jax.nn.softmax(scores, axis=-1).astype(jnp.bfloat16)  137 us
    unnamed x1, blocking collectives  68.7 us
    dot_general x4, matrix products, attn_mlp_block(): jnp.einsum('cqhk,hkd->cqd', attended, w_proj, preferred_element_type=jnp....  67.4 us
    dot_general x2, matrix products, attn_mlp_block(): jnp.einsum('cqhk,cshk->chqs', proj_qkv[0], kv_all[0], preferred_element_t...  57.2 us
  transfers between devices with their start and end apart: 8, of which 6 were waited for; matrix products, arithmetic and copies ran while one was open for 0% of the time, Pallas kernels for 0%

commit v1 on v0

v1 whole, which is shorter than its diff:
```python
import functools

import jax
import jax.numpy as jnp
from jax import lax
from jax.experimental import pallas as pl
from jax.experimental.pallas import tpu as pltpu
from jax.sharding import PartitionSpec as P

KEEP_DIV = 8
LANES = 128
LOG2E = 1.4426950408889634
NEG = -3e38


def layer_norm(hidden):
    hid_f32 = hidden.astype(jnp.float32)
    centred = hid_f32 - jnp.mean(hid_f32, axis=-1, keepdims=True)
    row_var = jnp.mean(centred * centred, axis=-1, keepdims=True)
    return (centred * lax.rsqrt(row_var + 1e-6)).astype(jnp.bfloat16)


def lane_iota(shape):
    return lax.broadcasted_iota(jnp.int32, shape, len(shape) - 1)


def flash(q, kv_ref, n_keys, bk, scale, mask_ref=None):
    rows = q.shape[0]
    c = scale * LOG2E

    def body(step, carry):
        m, l, acc = carry
        start = pl.multiple_of(step * bk, bk)
        kv = kv_ref[pl.ds(start, bk), :]
        s = lax.dot_general(q, kv, (((1,), (1,)), ((), ())), preferred_element_type=jnp.float32)
        m_new = jnp.maximum(m, jnp.max(s, axis=1, keepdims=True))
        p = jnp.exp2(s * c - m_new * c)
        alpha = jnp.exp2((m - m_new) * c)
        l = l * alpha + jnp.sum(p, axis=1, keepdims=True)
        acc = acc * alpha + jnp.dot(p.astype(jnp.bfloat16), kv[:, :LANES], preferred_element_type=jnp.float32)
        return m_new, l, acc

    init = (jnp.full((rows, 1), NEG, jnp.float32), jnp.zeros((rows, 1), jnp.float32), jnp.zeros((rows, LANES), jnp.float32))
    return lax.fori_loop(0, n_keys // bk, body, init)


def wait_bytes(ref, sem):
    pltpu.make_async_copy(ref, ref, sem).wait()


def attention_kernel(n, rows_kv, decoder, scale, bq, bk, kvm_ref, qm_ref, om_ref, kv_s, q_s, o_s, kvx_s, kv_send, kv_recv, q_send, q_recv, o_send, o_recv):
    me = lax.axis_index('sp')
    groups = n // 4
    pair = me // 4

    barrier = pltpu.get_barrier_semaphore()

    def greet(i, _):
        pl.semaphore_signal(barrier, inc=1, device_id={'sp': lax.rem(me + i, n)}, device_id_type=pl.DeviceIdType.MESH)
        return 0

    lax.fori_loop(1, n, greet, 0)
    pl.semaphore_wait(barrier, n - 1)

    def send_q(k, _):
        to = lax.rem(me + 4 * k, n)
        pltpu.make_async_remote_copy(
            src_ref=qm_ref.at[to // 4], dst_ref=q_s.at[k], send_sem=q_send, recv_sem=q_recv,
            device_id={'sp': to}, device_id_type=pl.DeviceIdType.MESH).start()
        return 0

    def send_kv(i, _):
        to = lax.rem(me + i, n)
        pltpu.make_async_remote_copy(
            src_ref=kvm_ref.at[to // 4], dst_ref=kv_s.at[i], send_sem=kv_send, recv_sem=kv_recv,
            device_id={'sp': to}, device_id_type=pl.DeviceIdType.MESH).start()
        return 0

    lax.fori_loop(1, groups, send_q, 0)
    lax.fori_loop(1, n, send_kv, 0)
    q_s[0] = qm_ref[pair]
    kv_s[0] = kvm_ref[pair]

    wait_bytes(q_s.at[pl.ds(1, groups - 1)], q_recv)
    wait_bytes(kv_s.at[pl.ds(1, n - 1)], kv_recv)

    n_rows = n * rows_kv
    kv = kv_s[...].reshape(n_rows, LANES)
    if decoder:
        kvx_s[...] = kv
    else:
        bad = kv == jnp.inf
        kvx_s[:, :LANES] = jnp.where(bad, 0, kv).astype(jnp.bfloat16)
        kvx_s[:, LANES:] = jnp.where(bad & (lane_iota(kv.shape) == 0), NEG, 0.0).astype(jnp.bfloat16)

    per = bq // 16
    lane_sq = lane_iota((LANES, LANES))
    row_sq = lax.broadcasted_iota(jnp.int32, (LANES, LANES), 0)

    def send_o(k):
        to = lax.rem(me - 4 * k + n, n)
        pltpu.make_async_remote_copy(
            src_ref=o_s.at[k], dst_ref=om_ref.at[pair], send_sem=o_send, recv_sem=o_recv,
            device_id={'sp': to}, device_id_type=pl.DeviceIdType.MESH).start()

    def q_block(b, _):
        qp = q_s[pl.ds(b * per, per)].reshape(bq, LANES)
        if decoder:
            parts = []
            for half in range(2):
                for j in range(4):
                    pick = ((row_sq - 32 * j == lane_sq - 64 * half) & (lane_sq >= 64 * half) & (lane_sq < 64 * half + 32)).astype(jnp.bfloat16)
                    parts.append(jnp.dot(qp, pick, preferred_element_type=jnp.float32).astype(jnp.bfloat16))
            m, l, acc = flash(jnp.concatenate(parts, axis=0), kvx_s, n_rows, bk, scale)
            h = 4 * bq
            m_all = jnp.maximum(m[:h], m[h:])
            ea = jnp.exp2((m[:h] - m_all) * (scale * LOG2E))
            eb = jnp.exp2((m[h:] - m_all) * (scale * LOG2E))
            denom = l[:h] * ea + l[h:] * eb
            out = (acc[:h] * ea + pltpu.roll(acc[h:], 64, 1) * eb) / denom
            lane = lane_iota((bq, LANES))
            packed = jnp.zeros((bq, LANES), jnp.float32)
            for j in range(4):
                part = out[j * bq:(j + 1) * bq]
                moved = part if j == 1 else pltpu.roll(part, (32 * (j - 1)) % LANES, 1)
                packed = jnp.where((lane >= 32 * j) & (lane < 32 * j + 32), moved, packed)
        else:
            ones = (lane_iota((bq, LANES)) == 0).astype(jnp.bfloat16)
            m, l, acc = flash(jnp.concatenate([qp, ones], axis=1), kvx_s, n_rows, bk, scale)
            packed = acc / l
        o_s[pl.ds(b * per, per)] = packed.astype(jnp.bfloat16).reshape(per, 16, LANES)

        @pl.when(b > 0)
        def _():
            for r in range(per):
                k = (b - 1) * per + r

                @pl.when(k > 0)
                def _():
                    send_o(k)
        return 0

    n_blocks = groups // per
    lax.fori_loop(0, n_blocks, q_block, 0)
    om_ref[pair] = o_s[0]
    for r in range(per):
        send_o((n_blocks - 1) * per + r)

    rest = o_s.at[pl.ds(1, groups - 1)]
    wait_bytes(rest, o_recv)
    wait_bytes(rest, o_send)
    wait_bytes(q_s.at[pl.ds(1, groups - 1)], q_send)
    wait_bytes(kv_s.at[pl.ds(1, n - 1)], kv_send)


def exchange_attention(kvm, qm, n, decoder, scale, bq, bk):
    groups, rows_kv = kvm.shape[0], kvm.shape[1]
    n_keys = n * rows_kv
    width = LANES if decoder else 2 * LANES
    q_rows = groups * 16 * (8 if decoder else 1)
    vmem = pl.BlockSpec(memory_space=pltpu.VMEM)
    return pl.pallas_call(
        functools.partial(attention_kernel, n, rows_kv, decoder, scale, bq, bk),
        out_shape=jax.ShapeDtypeStruct((groups, 16, LANES), jnp.bfloat16),
        in_specs=[vmem, vmem],
        out_specs=vmem,
        scratch_shapes=[
            pltpu.VMEM((n, rows_kv, LANES), jnp.bfloat16),
            pltpu.VMEM((groups, 16, LANES), jnp.bfloat16),
            pltpu.VMEM((groups, 16, LANES), jnp.bfloat16),
            pltpu.VMEM((n_keys, width), jnp.bfloat16),
        ] + [pltpu.SemaphoreType.DMA] * 6,
        compiler_params=pltpu.CompilerParams(
            collective_id=0 if decoder else 1, has_side_effects=True, vmem_limit_bytes=48 * 1024 * 1024),
        cost_estimate=pl.CostEstimate(flops=4 * q_rows * n_keys * LANES, bytes_accessed=2 * n_keys * LANES * 2, transcendentals=q_rows * n_keys),
        name='dec_attention' if decoder else 'enc_attention',
    )(kvm, qm)


def mlp(mid_state, w_up, w_down):
    up_act = jax.nn.gelu(jnp.dot(layer_norm(mid_state), w_up, preferred_element_type=jnp.float32), approximate=False).astype(jnp.bfloat16)
    return (mid_state + jnp.dot(up_act, w_down, preferred_element_type=jnp.float32)).astype(jnp.bfloat16)


def enc_block(hidden, valid, w_qkv, w_proj, w_up, w_down, n):
    clips, slots = valid.shape
    heads, hd = w_qkv.shape[2], w_qkv.shape[3]
    d = heads * hd
    qkv = jnp.dot(layer_norm(hidden), w_qkv.reshape(d, 3 * d), preferred_element_type=jnp.float32).astype(jnp.bfloat16)
    qkv = qkv.reshape(clips, slots, 3, heads, hd)
    kv = jnp.concatenate([qkv[:, :, 1], qkv[:, :, 2]], axis=-1)
    kv = jnp.where(valid[:, :, None, None], kv, jnp.inf).transpose(0, 2, 1, 3).reshape(clips * heads, slots, LANES)
    q = jnp.pad(qkv[:, :, 0], ((0, 0), (0, 0), (0, 0), (0, LANES - hd))).transpose(0, 2, 1, 3).reshape(clips * heads, slots, LANES)
    om = exchange_attention(kv, q, n, False, hd ** -0.5, 256, 1024)
    att = om.reshape(clips, heads, slots, LANES)[:, :, :, hd:].transpose(0, 2, 1, 3).reshape(clips * slots, d)
    mid = (hidden + jnp.dot(att, w_proj.reshape(d, d), preferred_element_type=jnp.float32)).astype(jnp.bfloat16)
    return mlp(mid, w_up, w_down)


def dec_block(hidden, clips, w_qkv, w_proj, w_up, w_down, n):
    rows = hidden.shape[0] // clips
    heads, hd = w_qkv.shape[2], w_qkv.shape[3]
    d = heads * hd
    qkv = jnp.dot(layer_norm(hidden), w_qkv.reshape(d, 3 * d), preferred_element_type=jnp.float32).astype(jnp.bfloat16)
    qkv = qkv.reshape(clips, rows, 3, heads, hd)
    kv = jnp.concatenate([qkv[:, :, 1], qkv[:, :, 2]], axis=-1)
    kv = kv.reshape(clips, 2, rows // 2, heads, 2 * hd).transpose(0, 3, 2, 1, 4).reshape(clips * heads, rows // 2, LANES)
    q = qkv[:, :, 0].reshape(clips, 4, rows // 4, heads, hd).transpose(0, 3, 2, 1, 4).reshape(clips * heads, rows // 4, LANES)
    om = exchange_attention(kv, q, n, True, hd ** -0.5, 64, 1024)
    att = om.reshape(clips, heads, rows // 4, 4, hd).transpose(0, 3, 2, 1, 4).reshape(clips * rows, d)
    mid = (hidden + jnp.dot(att, w_proj.reshape(d, d), preferred_element_type=jnp.float32)).astype(jnp.bfloat16)
    return mlp(mid, w_up, w_down)


def solution(mesh):
    n = mesh.shape['sp']

    def local_program(patches, vis_mask, enc_pos, dec_pos, w_pe, b_pe, enc_qkv, enc_proj, enc_up, enc_down, w_ed, mask_token, dec_qkv, dec_proj, dec_up, dec_down, w_out):
        clips, tokens = vis_mask.shape
        slots = 2 * (tokens // KEEP_DIV)
        upto = (jnp.arange(tokens)[:, None] < jnp.arange(tokens)[None, :]).astype(jnp.float32)
        local_rank = jnp.dot(vis_mask.astype(jnp.float32), upto).astype(jnp.int32)
        count = jnp.sum(vis_mask, axis=1)
        valid = jnp.arange(slots)[None, :] < count[:, None]
        select = ((local_rank[:, None, :] == jnp.arange(slots)[None, :, None]) & (vis_mask[:, None, :] == 1)).astype(jnp.bfloat16)
        moved_x = jnp.einsum('cqi,cip->cqp', select, patches, preferred_element_type=jnp.float32).astype(jnp.bfloat16)
        moved_pos = jnp.einsum('cqi,id->cqd', select, enc_pos, preferred_element_type=jnp.float32)
        hidden = (jnp.einsum('cqp,pd->cqd', moved_x, w_pe, preferred_element_type=jnp.float32)
                  + b_pe.astype(jnp.float32) + moved_pos).astype(jnp.bfloat16).reshape(clips * slots, -1)
        for layer in range(enc_qkv.shape[0]):
            hidden = enc_block(hidden, valid, enc_qkv[layer], enc_proj[layer], enc_up[layer], enc_down[layer], n)
        z = jnp.dot(layer_norm(hidden), w_ed, preferred_element_type=jnp.float32).astype(jnp.bfloat16)
        placed = jnp.einsum('cqi,cqe->cie', select, z.reshape(clips, slots, -1), preferred_element_type=jnp.float32)
        masked_part = (1 - vis_mask).astype(jnp.float32)[:, :, None] * mask_token.astype(jnp.float32)
        hidden = (placed + masked_part + dec_pos.astype(jnp.float32)).astype(jnp.bfloat16).reshape(clips * tokens, -1)
        for layer in range(dec_qkv.shape[0]):
            hidden = dec_block(hidden, clips, dec_qkv[layer], dec_proj[layer], dec_up[layer], dec_down[layer], n)
        return jnp.dot(layer_norm(hidden), w_out, preferred_element_type=jnp.float32).reshape(clips, tokens, -1)

    row_spec = P('dp', 'sp', None)
    pos_spec = P(('dp', 'sp'), None)
    arg_specs = (row_spec, P('dp', 'sp'), pos_spec, pos_spec) + (P(),) * 13
    return jax.shard_map(local_program, mesh=mesh, in_specs=arg_specs, out_specs=row_spec, check_vma=False)
```

time: 1660 us -> 279 us (0.17)
  waiting for transfers between devices: 777 us -> 0 us
  local copies, waits for them, and re-layouts: 450 us -> 30.4 us
  Pallas kernels: 0 us -> 195 us
  matrix products: 183 us -> 43.6 us
  other arithmetic: 144 us -> 8.3 us
  blocking collectives: 68.7 us -> 0 us
    all_gather x4 -> x0, waiting for transfers between devices: 771 us -> none  [attn_mlp_block(): kv_all = lax.all_gather(proj_qkv[1:], 'sp', axis=2, tiled=True)]
    unnamed x40 -> x20, local copies, waits for them, and re-layouts: 266 us -> 0.26 us
    pallas_call x0 -> x4, Pallas kernels: none -> 195 us  [exchange_attention(): pl.pallas_call(functools.partial(attention_kernel, n, rows_kv, decoder, s...]
    slice x10 -> x16, local copies, waits for them, and re-layouts: 184 us -> 20.9 us  [the longest x1 8.6 us: local_program(): enc_qkv[layer]]
    sub x2 -> x0, other arithmetic: 137 us -> none  [attn_mlp_block(): attn_probs = jax.nn.softmax(scores, axis=-1).astype(jnp.bfloat16)]
    dot_general x21 -> x16, matrix products: 169 us -> 41.1 us  [the longest x4 27.1 us: mlp(): jnp.dot(up_act, w_down, preferred_element_type=jnp.float32)]
    unnamed x1 -> x0, blocking collectives: 68.7 us -> none
  transfers between devices with their start and end apart: 8 -> 0, of which waited for: 6 -> 0; matrix products, arithmetic and copies ran while one was open for 0% -> 0% of each run, Pallas kernels for 0% -> 0%
where the time goes in v1:
time: 279 us; the launch traced here: 278 us
  Pallas kernels  195 us (70%)
  matrix products  43.6 us (16%)
  local copies, waits for them, and re-layouts  30.4 us (11%)
  other arithmetic  8.3 us (3%)
    pallas_call x4, Pallas kernels, exchange_attention(): pl.pallas_call(functools.partial(attention_kernel, n, rows_kv, decoder, s...  195 us
    dot_general x4, matrix products, mlp(): jnp.dot(up_act, w_down, preferred_element_type=jnp.float32)  27.1 us
    slice x1, local copies, waits for them, and re-layouts, local_program(): enc_qkv[layer]  8.6 us
    dot_general x2, matrix products, enc_block(): jnp.dot(layer_norm(hidden), w_qkv.reshape(d, 3 * d), preferred_element_ty...  6.68 us

profile of v1, /device:TPU:1, one launch (start us, length us, event | category | flops | bytes accessed | tf_op | source)
XLA Modules:
  0.0 278.4 jit_solution(9952831030136445176)
XLA Ops:
  0.0 0.9 fusion.78
  0.9 0.7 broadcast_compare_fusion
  1.6 0.7 convert_element_type.183
  2.3 1.4 fusion.51
  3.7 1.1 fusion.423
  5.1 8.6 %fusion.415 = (bf16[1,1024,3,16,64]{1,4,3,2,0:T(8,128)(2,1)}, bf16[1,1024,3,16,64]{1,4,3,2,0:T(8,128)(2,1)S(1)}) fusion(bf16[2,1024,3,16,64]{1,4,3,2,0:T(8,128)(2,1)} %param.23), kind=kLoop, calls=%fused_computation.467 | loop fusion | bytes 25165824 | tf_op jit(solution)/shard_map/slice | solution.py:231
  13.7 1.9 convolution_convert_fusion.1
  16.5 31.7 %enc_attention.2 = bf16[32,16,128]{2,1,0:T(8,128)(2,1)S(1)} custom-call(bf16[32,16,128]{2,1,0:T(8,128)(2,1)S(1)} %bitcast.205, bf16[32,16,128]{2,1,0:T(8,128)(2,1)S(1)} %bitcast.207), custom_call_target="tpu_custom_call" | custom-call | flops 536870912 | bytes 1048576 | tf_op jit(solution)/shard_map/enc_attention/pallas_call | solution.py:162
  48.5 4.2 %fusion.416 = (bf16[1,16,64,1024]{3,2,1,0:T(8,128)(2,1)}, bf16[1,16,64,1024]{3,2,1,0:T(8,128)(2,1)S(1)}) fusion(bf16[2,16,64,1024]{3,2,1,0:T(8,128)(2,1)} %param.24), kind=kLoop, calls=%fused_computation.468 | loop fusion | bytes 8388608 | tf_op jit(solution)/shard_map/slice | solution.py:231
  52.6 0.6 fusion.424
  53.4 8.1 %fusion.425 = (f32[32]{0:T(128)S(1)}, f32[32,1024]{1,0:T(8,128)S(1)}) fusion(f32[32,1024]{1,0:T(8,128)S(1)} %get-tuple-element.30, bf16[2,4096,1024]{2,1,0:T(8,128)(2,1)} %param.26, bf16[2,1024,4096]{2,1,0:T(8,128)(2,1)} %param.25, f32[32]{0:T(128)S(1)} %add_rsqrt_fusion.9, f32[32]{0:T(128)S(1)} %broadcast_multiply_fusion.9), kind=kOutput, calls=%fused_computation.477 | convolution fusion | flops 545619968 | bytes 17171584 | tf_op jit(solution)/shard_map/dot_general | solution.py:182
  61.7 4.7 %convolution_convert_fusion = bf16[32,3072]{1,0:T(8,128)(2,1)S(1)} fusion(bf16[1024,3072]{0,1:T(8,128)(2,1)} %bitcast.211, f32[32,1024]{1,0:T(8,128)S(1)} %get-tuple-element.32, f32[32]{0:T(128)S(1)} %add_rsqrt_fusion.8, f32[32]{0:T(128)S(1)} %broadcast_multiply_fusion.8), kind=kOutput, calls=%fused_computation.12 | convolution fusion | flops 201523200 | bytes 6619392 | tf_op jit(solution)/shard_map/dot_general | solution.py:189
  67.1 25.6 %enc_attention.3 = bf16[32,16,128]{2,1,0:T(8,128)(2,1)S(1)} custom-call(bf16[32,16,128]{2,1,0:T(8,128)(2,1)S(1)} %bitcast.204, bf16[32,16,128]{2,1,0:T(8,128)(2,1)S(1)} %bitcast.206), custom_call_target="tpu_custom_call" | custom-call | flops 536870912 | bytes 1048576 | tf_op jit(solution)/shard_map/enc_attention/pallas_call | solution.py:162
  93.0 2.2 fusion.428
  95.4 8.4 %fusion.429 = (f32[32]{0:T(128)S(1)}, f32[32,1024]{1,0:T(8,128)S(1)}) fusion(f32[32,1024]{1,0:T(8,128)S(1)} %get-tuple-element.34, bf16[2,4096,1024]{2,1,0:T(8,128)(2,1)} %param.26, bf16[2,1024,4096]{2,1,0:T(8,128)(2,1)} %param.25, f32[32]{0:T(128)S(1)} %add_rsqrt_fusion.7, f32[32]{0:T(128)S(1)} %broadcast_multiply_fusion.7), kind=kOutput, calls=%fused_computation.479 | convolution fusion | flops 545619968 | bytes 17171584 | tf_op jit(solution)/shard_map/dot_general | solution.py:182
  105.0 2.2 fusion.417
  107.2 0.6 convolution_convert_fusion.3
  108.4 1.5 fusion.420
  110.3 1.0 concatenate.25
  111.4 2.7 maximum_bitcast_fusion
  114.0 0.7 copy.35
  115.0 1.5 copy.36
  117.2 69.4 %dec_attention.2 = bf16[32,16,128]{2,1,0:T(8,128)(2,1)S(1)} custom-call(bf16[32,32,128]{2,1,0:T(8,128)(2,1)S(1)} %reshape.286.kvm_ref, bf16[32,16,128]{2,1,0:T(8,128)(2,1)S(1)} %reshape.287.qm_ref), custom_call_target="tpu_custom_call" | custom-call | flops 8589934592 | bytes 2097152 | tf_op jit(solution)/shard_map/dec_attention/pallas_call | solution.py:162
  187.6 1.3 fusion.418
  189.4 5.3 %fusion.434 = (f32[128]{0:T(128)S(1)}, f32[128,512]{1,0:T(8,128)S(1)}) fusion(f32[128,512]{1,0:T(8,128)S(1)} %get-tuple-element.40, bf16[2,2048,512]{2,1,0:T(8,128)(2,1)} %param.32, bf16[2,512,2048]{2,1,0:T(8,128)(2,1)} %param.31, f32[128]{0:T(128)S(1)} %add_rsqrt_fusion.5, f32[128]{0:T(128)S(1)} %broadcast_multiply_fusion.5), kind=kOutput, calls=%fused_computation.482 | convolution fusion | flops 554368896 | bytes 4982272 | tf_op jit(solution)/shard_map/dot_general | solution.py:182
  194.9 0.7 convolution_convert_fusion.2
  196.1 0.8 fusion.419
  197.6 1.6 maximum_bitcast_fusion.1
  199.2 0.7 copy.42
  201.3 68.7 %dec_attention.3 = bf16[32,16,128]{2,1,0:T(8,128)(2,1)S(1)} custom-call(bf16[32,32,128]{2,1,0:T(8,128)(2,1)S(1)} %reshape.291.kvm_ref, bf16[32,16,128]{2,1,0:T(8,128)(2,1)S(1)} %reshape.292.qm_ref), custom_call_target="tpu_custom_call" | custom-call | flops 8589934592 | bytes 2097152 | tf_op jit(solution)/shard_map/dec_attention/pallas_call | solution.py:162
  271.7 5.4 %fusion.438 = (f32[128]{0:T(128)S(1)}, f32[128,512]{1,0:T(8,128)S(1)}) fusion(f32[128,512]{1,0:T(8,128)S(1)} %get-tuple-element.44, bf16[2,2048,512]{2,1,0:T(8,128)(2,1)} %param.32, bf16[2,512,2048]{2,1,0:T(8,128)(2,1)} %param.31, f32[128]{0:T(128)S(1)} %add_rsqrt_fusion.3, f32[128]{0:T(128)S(1)} %broadcast_multiply_fusion.3), kind=kOutput, calls=%fused_computation.484 | convolution fusion | flops 554368896 | bytes 4982272 | tf_op jit(solution)/shard_map/dot_general | solution.py:182
  277.3 1.1 fusion.255
  (97 shorter events, 11.8 us)
Async XLA Ops:
  0.0 2.3 copy-start
  13.7 2.4 copy-start.6
  95.4 8.6 %copy-start.2 = (bf16[1024,512]{1,0:T(8,128)(2,1)S(1)}, bf16[1024,512]{1,0:T(8,128)(2,1)}, u32[]{:S(2)}) copy-start(bf16[1024,512]{1,0:T(8,128)(2,1)} %param.27) | copy-start | bytes 3145732
  95.4 8.9 %copy-start.4 = (bf16[64,512]{1,0:T(8,128)(2,1)S(1)}, bf16[64,512]{1,0:T(8,128)(2,1)}, u32[]{:S(2)}) copy-start(bf16[64,512]{1,0:T(8,128)(2,1)} %param.20) | copy-start | bytes 196612
  95.4 9.0 %copy-start.5 = (bf16[512]{0:T(512)(128)(2,1)S(1)}, bf16[512]{0:T(512)(128)(2,1)}, u32[]{:S(2)}) copy-start(bf16[512]{0:T(512)(128)(2,1)} %param.28) | copy-start | bytes 3076
  271.7 5.6 %copy-start.3 = (bf16[512,768]{1,0:T(8,128)(2,1)S(1)}, bf16[512,768]{1,0:T(8,128)(2,1)}, u32[]{:S(2)}) copy-start(bf16[512,768]{1,0:T(8,128)(2,1)} %param.33) | copy-start | bytes 2359300
  271.7 6.7 %copy-start.1 = (bf16[768,1024]{1,0:T(8,128)(2,1)S(1)}, bf16[768,1024]{1,0:T(8,128)(2,1)}, u32[]{:S(2)}) copy-start(bf16[768,1024]{1,0:T(8,128)(2,1)} %param.21) | copy-start | bytes 4718596

commit v2 on v0

v2 whole, which is shorter than its diff:
```python
import functools

import jax
import jax.numpy as jnp
from jax import lax
from jax.experimental import pallas as pl
from jax.experimental.pallas import tpu as pltpu
from jax.sharding import PartitionSpec as P

KEEP_DIV = 8
LANES = 128
QUARTERS = 4
MSG = 16
LOG2E = 1.4426950408889634
NEG = -3e38
BF16 = jnp.bfloat16
F32 = jnp.float32


def layer_norm(hidden):
    hid_f32 = hidden.astype(F32)
    centred = hid_f32 - jnp.mean(hid_f32, axis=-1, keepdims=True)
    row_var = jnp.mean(centred * centred, axis=-1, keepdims=True)
    return (centred * lax.rsqrt(row_var + 1e-6)).astype(BF16)


def gelu(x):
    return 0.5 * x * (1.0 + lax.erf(x * (0.5 ** 0.5)))


def dot(a, b):
    return jnp.dot(a, b, preferred_element_type=F32)


def dot_t(a, b):
    return lax.dot_general(a, b, (((1,), (1,)), ((), ())), preferred_element_type=F32)


def lane_of(shape):
    return lax.broadcasted_iota(jnp.int32, shape, len(shape) - 1)


def roll(x, shift):
    shift = shift % LANES
    return x if shift == 0 else pltpu.roll(x, shift, 1)


def wait_bytes(ref, sem):
    pltpu.make_async_copy(ref, ref, sem).wait()


def model_kernel(n, enc_heads, dec_heads, patches, mask, enc_pos, dec_pos, b_pe, mask_token,
                 w_pe, e_qkv, e_proj, e_up, e_down, w_ed, d_qkv, d_proj, d_up, d_down, w_out, out,
                 w_pe_s, e_qkv_s, e_proj_s, e_up_s, e_down_s, w_ed_s, d_qkv_s, d_proj_s, d_up_s, d_down_s, w_out_s,
                 ekvm, dkvm, qm, o_s, ekv, dkv, q_in, o_in, ekvx, kvt, qq, s_buf, p_buf, hid_e, qkv_e, att_e, hid_d, qkv_d, att_d, pick_s,
                 wsem, kv_send, kv_recv, q_send, q_recv, o_send, o_recv):
    me = lax.axis_index('sp')
    groups = n // QUARTERS
    pair = me // QUARTERS
    clips, tokens, _ = patches.shape
    slots = 2 * (tokens // KEEP_DIV)
    layers = e_qkv.shape[0]
    d_enc = enc_pos.shape[1]
    d_dec = dec_pos.shape[1]
    mesh_id = pl.DeviceIdType.MESH

    def load(src, dst, i):
        return pltpu.make_async_copy(src, dst, wsem.at[i])

    load_pe = load(w_pe, w_pe_s, 0)
    load_ed = load(w_ed, w_ed_s, 5)
    load_out = load(w_out, w_out_s, 10)
    enc_loads = [(e_qkv, e_qkv_s, 1), (e_proj, e_proj_s, 2), (e_up, e_up_s, 3), (e_down, e_down_s, 4)]
    dec_loads = [load(d_qkv, d_qkv_s, 6), load(d_proj, d_proj_s, 7), load(d_up, d_up_s, 8), load(d_down, d_down_s, 9)]

    def enc_load(which, layer):
        src, dst, i = enc_loads[which]
        return load(src.at[layer], dst, i)

    load_pe.start()
    enc_load(0, 0).start()

    barrier = pltpu.get_barrier_semaphore()

    def greet(i, _):
        pl.semaphore_signal(barrier, inc=1, device_id={'sp': lax.rem(me + i, n)}, device_id_type=mesh_id)
        return 0

    lax.fori_loop(1, n, greet, 0)

    mask_f = mask[...].astype(F32)
    before = lax.broadcasted_iota(jnp.int32, (tokens, tokens), 0) < lax.broadcasted_iota(jnp.int32, (tokens, tokens), 1)
    rank = dot(mask_f.astype(BF16), before.astype(BF16))
    slot_id = lax.broadcasted_iota(jnp.int32, (slots, tokens), 0).astype(F32)
    selects, moved_x, moved_pos, occupied = [], [], [], []
    for c in range(clips):
        select = jnp.where((rank[c:c + 1] == slot_id) & (mask_f[c:c + 1] > 0), 1.0, 0.0)
        selects.append(select)
        moved_x.append(dot(select.astype(BF16), patches[c]).astype(BF16))
        moved_pos.append(dot(select.astype(BF16), enc_pos[...]))
        occupied.append(jnp.sum(select, axis=1, keepdims=True))
    load_pe.wait()
    embedded = dot(jnp.concatenate(moved_x, axis=0), w_pe_s[...]) + b_pe[...].astype(F32) + jnp.concatenate(moved_pos, axis=0)
    hid_e[...] = embedded.astype(BF16)
    for which in range(1, 4):
        enc_load(which, 0).start()
    pl.semaphore_wait(barrier, n - 1)

    def exchange(phase, kvm, kv):
        def send_kv(i, _):
            to = lax.rem(me + i, n)
            pltpu.make_async_remote_copy(
                src_ref=kvm.at[to // QUARTERS], dst_ref=kv.at[i], send_sem=kv_send.at[phase], recv_sem=kv_recv.at[phase],
                device_id={'sp': to}, device_id_type=mesh_id).start()
            return 0

        def send_q(k, _):
            to = lax.rem(me + QUARTERS * k, n)
            pltpu.make_async_remote_copy(
                src_ref=qm.at[to // QUARTERS], dst_ref=q_in.at[phase, k], send_sem=q_send.at[phase], recv_sem=q_recv.at[phase],
                device_id={'sp': to}, device_id_type=mesh_id).start()
            return 0

        lax.fori_loop(1, groups, send_q, 0)
        lax.fori_loop(1, n, send_kv, 0)
        q_in[phase, 0] = qm[pair]
        kv[0] = kvm[pair]

    def arrived(phase, kv):
        wait_bytes(q_in.at[phase, pl.ds(1, groups - 1)], q_recv.at[phase])
        wait_bytes(kv.at[pl.ds(1, n - 1)], kv_recv.at[phase])

    def send_home(phase, k):
        to = lax.rem(me - QUARTERS * k + n, n)
        pltpu.make_async_remote_copy(
            src_ref=o_s.at[k], dst_ref=o_in.at[phase, pair], send_sem=o_send.at[phase], recv_sem=o_recv.at[phase],
            device_id={'sp': to}, device_id_type=mesh_id).start()

    def finish(phase, kv):
        rest = pl.ds(1, groups - 1)
        wait_bytes(o_in.at[phase, rest], o_recv.at[phase])
        wait_bytes(o_s.at[rest], o_send.at[phase])
        wait_bytes(qm.at[rest], q_send.at[phase])
        wait_bytes(kv.at[pl.ds(1, n - 1)], kv_send.at[phase])

    hd_e = d_enc // enc_heads
    lane_e = lane_of((slots, LANES))
    c_e = hd_e ** -0.5 * LOG2E
    n_e = n * slots
    m_e = groups * slots
    bk = 256

    def enc_layer(layer, _):
        normed = layer_norm(hid_e[...])
        enc_load(0, layer).wait()
        for t in range(0, 3 * d_enc, 1024):
            qkv_e[:, t:t + 1024] = dot_t(normed, e_qkv_s[t:t + 1024])

        @pl.when(layer + 1 < layers)
        def _():
            enc_load(0, layer + 1).start()

        for c in range(clips):
            rows = slice(c * slots, (c + 1) * slots)
            for h in range(enc_heads):
                tile = (h * hd_e) // LANES * LANES
                off = h * hd_e - tile
                q_t = roll(qkv_e[rows, tile:tile + LANES], -off)
                k_t = roll(qkv_e[rows, d_enc + tile:d_enc + tile + LANES], -off)
                v_t = roll(qkv_e[rows, 2 * d_enc + tile:2 * d_enc + tile + LANES], hd_e - off)
                qm[c * enc_heads + h] = jnp.where(lane_e < hd_e, q_t, 0.0).astype(BF16)
                kv_t = jnp.where(lane_e < hd_e, k_t, v_t)
                ekvm[c * enc_heads + h] = jnp.where(occupied[c] > 0, kv_t, jnp.inf).astype(BF16)

        kv = ekv.at[layer]
        exchange(layer, ekvm, kv)

        @pl.when(layer == 0)
        def _():
            load_ed.start()
            for copy in dec_loads:
                copy.start()
            load_out.start()

        arrived(layer, kv)
        for t in range(0, n, 32):
            block = kv[t:t + 32].reshape(32 * slots, LANES)
            bad = block == jnp.inf
            r = slice(t * slots, (t + 32) * slots)
            clean = jnp.where(bad, jnp.zeros_like(block), block)
            ekvx[r, :LANES] = clean
            ekvx[r, LANES:] = jnp.where(bad & (lane_of(block.shape) == 0), jnp.full_like(block, NEG), jnp.zeros_like(block))
            kvt[:, r] = clean.T
        q = q_in[layer].reshape(m_e, LANES)
        q = jnp.concatenate([q, (lane_of(q.shape) == 0).astype(BF16)], axis=1)
        steps = n_e // bk
        m = jnp.full((1, m_e), NEG, F32)
        l = jnp.zeros((1, m_e), F32)
        acc = jnp.zeros((hd_e, m_e), F32)
        s_buf[0, :, :m_e] = dot_t(ekvx[:bk], q)
        prev = None
        for i in range(steps):
            if i + 1 < steps:
                s_buf[(i + 1) % 2, :, :m_e] = dot_t(ekvx[(i + 1) * bk:(i + 2) * bk], q)
            s = s_buf[i % 2, :, :m_e]
            m_new = jnp.maximum(m, jnp.max(s, axis=0, keepdims=True))
            p = jnp.exp2(s * c_e - m_new * c_e)
            alpha = jnp.exp2((m - m_new) * c_e)
            l = l * alpha + jnp.sum(p, axis=0, keepdims=True)
            p_buf[i % 2, :, :m_e] = p.astype(BF16)
            m = m_new
            if prev is not None:
                j, a = prev
                acc = acc * a + dot(kvt[hd_e:2 * hd_e, j * bk:(j + 1) * bk], p_buf[j % 2, :, :m_e])
            prev = (i, alpha)
        j, a = prev
        acc = acc * a + dot(kvt[hd_e:2 * hd_e, j * bk:(j + 1) * bk], p_buf[j % 2, :, :m_e])
        res = acc / l
        odd = lax.rem(pair, 2) == 1
        zero = jnp.zeros_like(res)
        both = jnp.concatenate([jnp.where(odd, zero, res), jnp.where(odd, res, zero)], axis=0)
        o_s[...] = both.T.astype(BF16).reshape(groups, slots, LANES)

        def home(k, _):
            send_home(layer, k)
            return 0

        o_in[layer, pair] = o_s[0]
        lax.fori_loop(1, groups, home, 0)
        finish(layer, kv)

        for c in range(clips):
            for g in range(enc_heads // 2):
                first = c * enc_heads + 2 * g
                att_e[c * slots:(c + 1) * slots, g * LANES:(g + 1) * LANES] = (
                    o_in[layer, first].astype(F32) + o_in[layer, first + 1].astype(F32)).astype(BF16)
        enc_load(1, layer).wait()
        mid = (hid_e[...].astype(F32) + dot(att_e[...], e_proj_s[...])).astype(BF16)

        @pl.when(layer + 1 < layers)
        def _():
            enc_load(1, layer + 1).start()

        normed = layer_norm(mid)
        enc_load(2, layer).wait()
        enc_load(3, layer).wait()
        total = mid.astype(F32)
        for t in range(0, e_up_s.shape[1], 1024):
            up = gelu(dot(normed, e_up_s[:, t:t + 1024])).astype(BF16)
            total = total + dot(up, e_down_s[t:t + 1024])

        @pl.when(layer + 1 < layers)
        def _():
            enc_load(2, layer + 1).start()
            enc_load(3, layer + 1).start()

        hid_e[...] = total.astype(BF16)
        return 0

    lax.fori_loop(0, layers, enc_layer, 0)

    load_ed.wait()
    z = dot(layer_norm(hid_e[...]), w_ed_s[...]).astype(BF16)
    for c in range(clips):
        placed = lax.dot_general(selects[c].astype(BF16), z[c * slots:(c + 1) * slots], (((0,), (0,)), ((), ())), preferred_element_type=F32)
        seen = jnp.max(selects[c].T, axis=1, keepdims=True)
        token = jnp.where(seen > 0, placed, mask_token[...].astype(F32))
        hid_d[c * tokens:(c + 1) * tokens] = (token + dec_pos[...].astype(F32)).astype(BF16)

    hd_d = d_dec // dec_heads
    c_d = hd_d ** -0.5 * LOG2E
    half = tokens // 2
    parts = LANES // hd_d
    rows_q = tokens // parts
    n_d = n * half
    q_rows = groups * rows_q
    blk = 128
    m_d = 2 * parts * blk
    h_d = m_d // 2
    per = blk // rows_q
    lane_q = lane_of((rows_q, LANES))
    lane_k = lane_of((half, LANES))
    col = lane_of((LANES, 2 * parts * LANES))
    row = lax.broadcasted_iota(jnp.int32, col.shape, 0)
    part = col // LANES
    inside = lax.rem(col, LANES) - jnp.where(part >= parts, 2 * hd_d, 0)
    pick_s[...] = jnp.where((inside >= 0) & (inside < hd_d) & (row == inside + hd_d * lax.rem(part, parts)), 1.0, 0.0).astype(BF16)
    for copy in dec_loads:
        copy.wait()

    def dec_layer(layer, _):
        phase = layers + layer
        normed = layer_norm(hid_d[...])
        qkv_d[...] = dot_t(normed, d_qkv_s[layer])
        for c in range(clips):
            base = c * tokens
            for h in range(dec_heads):
                tile = (h * hd_d) // LANES * LANES
                off = h * hd_d - tile
                lo = slice(base, base + half)
                hi = slice(base + half, base + tokens)
                kc = slice(d_dec + tile, d_dec + tile + LANES)
                vc = slice(2 * d_dec + tile, 2 * d_dec + tile + LANES)
                k_lo, v_lo = roll(qkv_d[lo, kc], -off), roll(qkv_d[lo, vc], hd_d - off)
                k_hi, v_hi = roll(qkv_d[hi, kc], 2 * hd_d - off), roll(qkv_d[hi, vc], 3 * hd_d - off)
                dkvm[c * dec_heads + h] = jnp.where(
                    lane_k < 2 * hd_d, jnp.where(lane_k < hd_d, k_lo, v_lo), jnp.where(lane_k < 3 * hd_d, k_hi, v_hi)).astype(BF16)
                packed = None
                for j in range(parts):
                    moved = roll(qkv_d[base + j * rows_q:base + (j + 1) * rows_q, tile:tile + LANES], hd_d * j - off)
                    packed = moved if packed is None else jnp.where(lane_q >= hd_d * j, moved, packed)
                qm[c * dec_heads + h] = packed.astype(BF16)
        kv = dkv.at[layer]
        exchange(phase, dkvm, kv)
        arrived(phase, kv)

        spread = dot(q_in[phase].reshape(q_rows, LANES), pick_s[...])
        for b in range(q_rows // blk):
            for t in range(2 * parts):
                qq[b * m_d + t * blk:b * m_d + (t + 1) * blk] = spread[b * blk:(b + 1) * blk, t * LANES:(t + 1) * LANES].astype(BF16)
        for t in range(0, n, 16):
            kvt[:, t * half:(t + 16) * half] = kv[t:t + 16].reshape(16 * half, LANES).T

        steps = n_d // bk
        msgs = bk // half
        blocks = q_rows // blk

        def scores(b, i, slot):
            q = qq[pl.ds(pl.multiple_of(b * m_d, m_d), m_d)]
            s_buf[slot] = dot_t(kv[i * msgs:(i + 1) * msgs].reshape(bk, LANES), q)

        scores(0, 0, 0)

        def q_block(b, _):
            m = jnp.full((1, m_d), NEG, F32)
            l = jnp.zeros((1, m_d), F32)
            acc_a = jnp.zeros((hd_d, h_d), F32)
            acc_b = jnp.zeros((hd_d, h_d), F32)
            alphas = []

            def add(i, acc_a, acc_b):
                keys = slice(i * bk, (i + 1) * bk)
                acc_a = acc_a * alphas[i][:, :h_d] + dot(kvt[hd_d:2 * hd_d, keys], p_buf[i % 2, :, :h_d])
                acc_b = acc_b * alphas[i][:, h_d:] + dot(kvt[3 * hd_d:4 * hd_d, keys], p_buf[i % 2, :, h_d:])
                return acc_a, acc_b

            for i in range(steps):
                if i + 1 < steps:
                    scores(b, i + 1, (i + 1) % 2)
                else:
                    scores(jnp.minimum(b + 1, blocks - 1), 0, 0)
                s = s_buf[i % 2]
                m_new = jnp.maximum(m, jnp.max(s, axis=0, keepdims=True))
                p = jnp.exp2(s * c_d - m_new * c_d)
                alphas.append(jnp.exp2((m - m_new) * c_d))
                l = l * alphas[i] + jnp.sum(p, axis=0, keepdims=True)
                p_buf[i % 2] = p.astype(BF16)
                m = m_new
                if i > 0:
                    acc_a, acc_b = add(i - 1, acc_a, acc_b)
            acc_a, acc_b = add(steps - 1, acc_a, acc_b)
            m_all = jnp.maximum(m[:, :h_d], m[:, h_d:])
            e_a = jnp.exp2((m[:, :h_d] - m_all) * c_d)
            e_b = jnp.exp2((m[:, h_d:] - m_all) * c_d)
            res = (acc_a * e_a + acc_b * e_b) / (l[:, :h_d] * e_a + l[:, h_d:] * e_b)
            stacked = jnp.concatenate([res[:, j * blk:(j + 1) * blk] for j in range(parts)], axis=0)
            o_s[pl.ds(b * per, per)] = stacked.T.astype(BF16).reshape(per, rows_q, LANES)

            def home(k, _):
                send_home(phase, k)
                return 0

            lax.fori_loop(jnp.maximum(b * per, 1), (b + 1) * per, home, 0)
            return 0

        lax.fori_loop(0, blocks, q_block, 0)
        o_in[phase, pair] = o_s[0]
        finish(phase, kv)

        for c in range(clips):
            for g in range(dec_heads // parts):
                got = [o_in[phase, c * dec_heads + parts * g + h].astype(F32) for h in range(parts)]
                for j in range(parts):
                    tile = None
                    for h in range(parts):
                        moved = roll(got[h], hd_d * (h - j))
                        tile = moved if tile is None else jnp.where(lane_q >= hd_d * h, moved, tile)
                    att_d[c * tokens + j * rows_q:c * tokens + (j + 1) * rows_q, g * LANES:(g + 1) * LANES] = tile.astype(BF16)
        mid = (hid_d[...].astype(F32) + dot(att_d[...], d_proj_s[layer])).astype(BF16)
        up = gelu(dot(layer_norm(mid), d_up_s[layer])).astype(BF16)
        hid_d[...] = (mid.astype(F32) + dot(up, d_down_s[layer])).astype(BF16)
        return 0

    lax.fori_loop(0, layers, dec_layer, 0)
    load_out.wait()
    result = dot(layer_norm(hid_d[...]), w_out_s[...])
    for c in range(clips):
        out[c] = result[c * tokens:(c + 1) * tokens]


def solution(mesh):
    n = mesh.shape['sp']

    def local_program(patches, vis_mask, enc_pos, dec_pos, w_pe, b_pe, enc_qkv, enc_proj, enc_up, enc_down, w_ed, mask_token, dec_qkv, dec_proj, dec_up, dec_down, w_out):
        clips, tokens, width = patches.shape
        layers, d_enc, _, enc_heads, _ = enc_qkv.shape
        _, d_dec, _, dec_heads, _ = dec_qkv.shape
        slots = 2 * (tokens // KEEP_DIV)
        half = tokens // 2
        groups = n // QUARTERS
        f_enc, f_dec = enc_up.shape[2], dec_up.shape[2]
        e_rows, d_rows = clips * slots, clips * tokens
        phases = 2 * layers
        bk, m_d = 256, 1024
        vmem = pl.BlockSpec(memory_space=pltpu.VMEM)
        hbm = pl.BlockSpec(memory_space=pl.ANY)

        def buf(*shape, dtype=BF16):
            return pltpu.VMEM(shape, dtype)

        return pl.pallas_call(
            functools.partial(model_kernel, n, enc_heads, dec_heads),
            out_shape=jax.ShapeDtypeStruct((clips, tokens, w_out.shape[1]), F32),
            in_specs=[vmem] * 6 + [hbm] * 11,
            out_specs=vmem,
            scratch_shapes=[
                buf(width, d_enc), buf(3 * d_enc, d_enc), buf(d_enc, d_enc), buf(d_enc, f_enc), buf(f_enc, d_enc), buf(d_enc, d_dec),
                buf(layers, 3 * d_dec, d_dec), buf(layers, d_dec, d_dec), buf(layers, d_dec, f_dec), buf(layers, f_dec, d_dec), buf(d_dec, w_out.shape[1]),
                buf(groups, slots, LANES), buf(groups, half, LANES), buf(groups, MSG, LANES), buf(groups, MSG, LANES),
                buf(layers, n, slots, LANES), buf(layers, n, half, LANES), buf(phases, groups, MSG, LANES), buf(phases, groups, MSG, LANES),
                buf(n * slots, 2 * LANES), buf(LANES, n * half), buf(groups * MSG * 8, LANES),
                buf(2, bk, m_d, dtype=F32), buf(2, bk, m_d),
                buf(e_rows, d_enc), buf(e_rows, 3 * d_enc, dtype=F32), buf(e_rows, d_enc),
                buf(d_rows, d_dec), buf(d_rows, 3 * d_dec, dtype=F32), buf(d_rows, d_dec),
                buf(LANES, 8 * LANES),
                pltpu.SemaphoreType.DMA((11,)),
            ] + [pltpu.SemaphoreType.DMA((phases,))] * 6,
            compiler_params=pltpu.CompilerParams(collective_id=0, has_side_effects=True, vmem_limit_bytes=67043328),
            name='model',
        )(patches, vis_mask, enc_pos, dec_pos, b_pe.reshape(1, -1), mask_token.reshape(1, -1), w_pe,
          enc_qkv.transpose(0, 2, 3, 4, 1).reshape(layers, 3 * d_enc, d_enc), enc_proj.reshape(layers, d_enc, d_enc), enc_up, enc_down, w_ed,
          dec_qkv.transpose(0, 2, 3, 4, 1).reshape(layers, 3 * d_dec, d_dec), dec_proj.reshape(layers, d_dec, d_dec), dec_up, dec_down, w_out)

    row_spec = P('dp', 'sp', None)
    pos_spec = P(('dp', 'sp'), None)
    arg_specs = (row_spec, P('dp', 'sp'), pos_spec, pos_spec) + (P(),) * 13
    return jax.shard_map(local_program, mesh=mesh, in_specs=arg_specs, out_specs=row_spec, check_vma=False)
```

time: 1660 us -> 175 us (0.11)
  waiting for transfers between devices: 777 us -> 0 us
  local copies, waits for them, and re-layouts: 450 us -> 4.3 us
  matrix products: 183 us -> 0 us
  Pallas kernels: 0 us -> 171 us
  other arithmetic: 144 us -> 0 us
  blocking collectives: 68.7 us -> 0 us
    all_gather x4 -> x0, waiting for transfers between devices: 771 us -> none  [attn_mlp_block(): kv_all = lax.all_gather(proj_qkv[1:], 'sp', axis=2, tiled=True)]
    unnamed x40 -> x1, local copies, waits for them, and re-layouts: 266 us -> 1.77 us
    slice x10 -> x0, local copies, waits for them, and re-layouts: 184 us -> none  [the longest x2 177 us: attn_mlp_block(): kv_all[1]]
    dot_general x23 -> x0, matrix products: 171 us -> none  [the longest x4 67.4 us: attn_mlp_block(): jnp.einsum('cqhk,hkd->cqd', attended, w_proj, preferred_element_type=jnp....]
    pallas_call x0 -> x1, Pallas kernels: none -> 171 us  [local_program(): pl.pallas_call(functools.partial(model_kernel, n, enc_heads, dec_heads),...]
    sub x2 -> x0, other arithmetic: 137 us -> none  [attn_mlp_block(): attn_probs = jax.nn.softmax(scores, axis=-1).astype(jnp.bfloat16)]
    unnamed x1 -> x0, blocking collectives: 68.7 us -> none
  transfers between devices with their start and end apart: 8 -> 0, of which waited for: 6 -> 0; matrix products, arithmetic and copies ran while one was open for 0% -> 0% of each run, Pallas kernels for 0% -> 0%
where the time goes in v2:
time: 175 us
  Pallas kernels  171 us (98%)
  local copies, waits for them, and re-layouts  4.3 us (2%)
    pallas_call x1, Pallas kernels, local_program(): pl.pallas_call(functools.partial(model_kernel, n, enc_heads, dec_heads),...  171 us

profile of v2, /device:TPU:1, one launch (start us, length us, event | category | flops | bytes accessed | tf_op | source)
XLA Modules:
  0.0 175.1 jit_solution(117094451508654436)
XLA Ops:
  0.0 1.3 reshape.19.mask_token
  1.3 1.3 reshape.18.b_pe
  2.5 170.8 %model.1 = f32[2,64,768]{2,1,0:T(8,128)} custom-call(bf16[2,64,768]{2,1,0:T(8,128)(2,1)} %patches.1, s32[2,64]{1,0:T(2,128)} %mask.1, bf16[64,1024]{1,0:T(8,128)(2,1)} %enc_pos.1, bf16[64,512]{1,0:T(8,128)(2,1)} %dec_pos.1, bf16[1,1024]{1,0:T(2,128)(2,1)} %reshape.18.b_pe, bf16[1,512]{1,0:T(2,128)(2,1)} %reshape.19.mask_token, bf16[768,1024]{1,0:T(8,128)(2,1)} %w_pe.1, ...), custom_call_target="tpu_custom_call" | custom-call | tf_op jit(solution)/shard_map/model/pallas_call | solution.py:421
  173.4 1.8 %copy.19 = f32[2,64,768]{2,1,0:T(8,128)} copy(f32[2,64,768]{2,1,0:T(8,128)} %model.1) | data formatting | bytes 786432

commit v3 on v2

--- a/solution.py
+++ b/solution.py
@@ -13,6 +13,8 @@
 MSG = 16
 LOG2E = 1.4426950408889634
 NEG = -3e38
+SIDE = 4
+CHUNKS = 4
 BF16 = jnp.bfloat16
 F32 = jnp.float32
 
@@ -53,10 +55,27 @@
                  w_pe, e_qkv, e_proj, e_up, e_down, w_ed, d_qkv, d_proj, d_up, d_down, w_out, out,
                  w_pe_s, e_qkv_s, e_proj_s, e_up_s, e_down_s, w_ed_s, d_qkv_s, d_proj_s, d_up_s, d_down_s, w_out_s,
                  ekvm, dkvm, qm, o_s, ekv, dkv, q_in, o_in, ekvx, kvt, qq, s_buf, p_buf, hid_e, qkv_e, att_e, hid_d, qkv_d, att_d, pick_s,
-                 wsem, kv_send, kv_recv, q_send, q_recv, o_send, o_recv):
+                 m_st, l_st, acc_st, wsem, kv_send, kv_recv, f_send, f_recv, q_send, q_recv, o_send, o_recv):
     me = lax.axis_index('sp')
     groups = n // QUARTERS
     pair = me // QUARTERS
+    chips = n // 2
+    per_chunk = chips // CHUNKS
+    core = lax.rem(me, 2)
+    partner = me + 1 - 2 * core
+    at_z, at_y, at_x = me // 32, lax.rem(me // 8, SIDE), lax.rem(me // 2, SIDE)
+
+    def device_at(dz, dy, dx):
+        return (lax.rem(at_z + dz, SIDE) * SIDE + lax.rem(at_y + dy, SIDE)) * 8 + lax.rem(at_x + dx, SIDE) * 2 + core
+
+    far = {0: 0, 1: 1, 2: 2, 3: 1}
+    offsets = sorted(((dz, dy, dx) for dz in range(SIDE) for dy in range(SIDE) for dx in range(SIDE)), key=lambda o: far[o[0]] + far[o[1]] + far[o[2]])
+
+    def query_offset(block, j):
+        return 2 * lax.rem(block, 2) + j // 4, j % 4, 2 * (block // 2)
+
+    def back(d):
+        return SIDE - d
     clips, tokens, _ = patches.shape
     slots = 2 * (tokens // KEEP_DIV)
     layers = e_qkv.shape[0]
@@ -83,10 +102,11 @@
     barrier = pltpu.get_barrier_semaphore()
 
     def greet(i, _):
-        pl.semaphore_signal(barrier, inc=1, device_id={'sp': lax.rem(me + i, n)}, device_id_type=mesh_id)
+        pl.semaphore_signal(barrier, inc=1, device_id={'sp': lax.rem(me + 2 * i, n)}, device_id_type=mesh_id)
         return 0
 
-    lax.fori_loop(1, n, greet, 0)
+    lax.fori_loop(1, chips, greet, 0)
+    pl.semaphore_signal(barrier, inc=1, device_id={'sp': partner}, device_id_type=mesh_id)
 
     mask_f = mask[...].astype(F32)
     before = lax.broadcasted_iota(jnp.int32, (tokens, tokens), 0) < lax.broadcasted_iota(jnp.int32, (tokens, tokens), 1)
@@ -104,36 +124,39 @@
     hid_e[...] = embedded.astype(BF16)
     for which in range(1, 4):
         enc_load(which, 0).start()
-    pl.semaphore_wait(barrier, n - 1)
 
     def exchange(phase, kvm, kv):
-        def send_kv(i, _):
-            to = lax.rem(me + i, n)
-            pltpu.make_async_remote_copy(
-                src_ref=kvm.at[to // QUARTERS], dst_ref=kv.at[i], send_sem=kv_send.at[phase], recv_sem=kv_recv.at[phase],
-                device_id={'sp': to}, device_id_type=mesh_id).start()
-            return 0
-
-        def send_q(k, _):
-            to = lax.rem(me + QUARTERS * k, n)
+        for k in range(1, groups):
+            to = device_at(*query_offset(k // 8, k % 8))
             pltpu.make_async_remote_copy(
                 src_ref=qm.at[to // QUARTERS], dst_ref=q_in.at[phase, k], send_sem=q_send.at[phase], recv_sem=q_recv.at[phase],
                 device_id={'sp': to}, device_id_type=mesh_id).start()
-            return 0
-
-        lax.fori_loop(1, groups, send_q, 0)
-        lax.fori_loop(1, n, send_kv, 0)
+        for i in range(1, chips):
+            to = device_at(*offsets[i])
+            pltpu.make_async_remote_copy(
+                src_ref=kvm.at[to // QUARTERS], dst_ref=kv.at[i], send_sem=kv_send.at[phase], recv_sem=kv_recv.at[phase, i // per_chunk],
+                device_id={'sp': to}, device_id_type=mesh_id).start()
         q_in[phase, 0] = qm[pair]
         kv[0] = kvm[pair]
 
-    def arrived(phase, kv):
+    def relay(phase, kv, c):
+        first = 1 if c == 0 else 0
+        wait_bytes(kv.at[pl.ds(c * per_chunk + first, per_chunk - first)], kv_recv.at[phase, c])
+        pltpu.make_async_remote_copy(
+            src_ref=kv.at[pl.ds(c * per_chunk, per_chunk)], dst_ref=kv.at[pl.ds(chips + c * per_chunk, per_chunk)],
+            send_sem=f_send.at[phase], recv_sem=f_recv.at[phase, c], device_id={'sp': partner}, device_id_type=mesh_id).start()
+
+    def relayed(phase, kv, c):
+        wait_bytes(kv.at[pl.ds(chips + c * per_chunk, per_chunk)], f_recv.at[phase, c])
+
+    def queries_in(phase):
         wait_bytes(q_in.at[phase, pl.ds(1, groups - 1)], q_recv.at[phase])
-        wait_bytes(kv.at[pl.ds(1, n - 1)], kv_recv.at[phase])
-
-    def send_home(phase, k):
-        to = lax.rem(me - QUARTERS * k + n, n)
+
+    def send_home(phase, block, j):
+        dz, dy, dx = query_offset(block, j)
+        to = device_at(back(dz), back(dy), back(dx))
         pltpu.make_async_remote_copy(
-            src_ref=o_s.at[k], dst_ref=o_in.at[phase, pair], send_sem=o_send.at[phase], recv_sem=o_recv.at[phase],
+            src_ref=o_s.at[8 * block + j], dst_ref=o_in.at[phase, pair], send_sem=o_send.at[phase], recv_sem=o_recv.at[phase],
             device_id={'sp': to}, device_id_type=mesh_id).start()
 
     def finish(phase, kv):
@@ -141,7 +164,8 @@
         wait_bytes(o_in.at[phase, rest], o_recv.at[phase])
         wait_bytes(o_s.at[rest], o_send.at[phase])
         wait_bytes(qm.at[rest], q_send.at[phase])
-        wait_bytes(kv.at[pl.ds(1, n - 1)], kv_send.at[phase])
+        wait_bytes(kv.at[pl.ds(1, chips - 1)], kv_send.at[phase])
+        wait_bytes(kv.at[pl.ds(0, chips)], f_send.at[phase])
 
     hd_e = d_enc // enc_heads
     lane_e = lane_of((slots, LANES))
@@ -173,6 +197,11 @@
                 ekvm[c * enc_heads + h] = jnp.where(occupied[c] > 0, kv_t, jnp.inf).astype(BF16)
 
         kv = ekv.at[layer]
+
+        @pl.when(layer == 0)
+        def _():
+            pl.semaphore_wait(barrier, chips)
+
         exchange(layer, ekvm, kv)
 
         @pl.when(layer == 0)
@@ -182,7 +211,11 @@
                 copy.start()
             load_out.start()
 
-        arrived(layer, kv)
+        for c in range(CHUNKS):
+            relay(layer, kv, c)
+        queries_in(layer)
+        for c in range(CHUNKS):
+            relayed(layer, kv, c)
         for t in range(0, n, 32):
             block = kv[t:t + 32].reshape(32 * slots, LANES)
             bad = block == jnp.inf
@@ -221,12 +254,9 @@
         both = jnp.concatenate([jnp.where(odd, zero, res), jnp.where(odd, res, zero)], axis=0)
         o_s[...] = both.T.astype(BF16).reshape(groups, slots, LANES)
 
-        def home(k, _):
-            send_home(layer, k)
-            return 0
-
         o_in[layer, pair] = o_s[0]
-        lax.fori_loop(1, groups, home, 0)
+        for k in range(groups - 1, 0, -1):
+            send_home(layer, k // 8, k % 8)
         finish(layer, kv)
 
         for c in range(clips):
@@ -312,68 +342,84 @@
                 qm[c * dec_heads + h] = packed.astype(BF16)
         kv = dkv.at[layer]
         exchange(phase, dkvm, kv)
-        arrived(phase, kv)
-
+        relay(phase, kv, 0)
+        queries_in(phase)
         spread = dot(q_in[phase].reshape(q_rows, LANES), pick_s[...])
         for b in range(q_rows // blk):
             for t in range(2 * parts):
                 qq[b * m_d + t * blk:b * m_d + (t + 1) * blk] = spread[b * blk:(b + 1) * blk, t * LANES:(t + 1) * LANES].astype(BF16)
-        for t in range(0, n, 16):
-            kvt[:, t * half:(t + 16) * half] = kv[t:t + 16].reshape(16 * half, LANES).T
-
-        steps = n_d // bk
+
         msgs = bk // half
         blocks = q_rows // blk
-
-        def scores(b, i, slot):
-            q = qq[pl.ds(pl.multiple_of(b * m_d, m_d), m_d)]
-            s_buf[slot] = dot_t(kv[i * msgs:(i + 1) * msgs].reshape(bk, LANES), q)
-
-        scores(0, 0, 0)
-
-        def q_block(b, _):
-            m = jnp.full((1, m_d), NEG, F32)
-            l = jnp.zeros((1, m_d), F32)
-            acc_a = jnp.zeros((hd_d, h_d), F32)
-            acc_b = jnp.zeros((hd_d, h_d), F32)
-            alphas = []
-
-            def add(i, acc_a, acc_b):
-                keys = slice(i * bk, (i + 1) * bk)
-                acc_a = acc_a * alphas[i][:, :h_d] + dot(kvt[hd_d:2 * hd_d, keys], p_buf[i % 2, :, :h_d])
-                acc_b = acc_b * alphas[i][:, h_d:] + dot(kvt[3 * hd_d:4 * hd_d, keys], p_buf[i % 2, :, h_d:])
-                return acc_a, acc_b
-
-            for i in range(steps):
-                if i + 1 < steps:
-                    scores(b, i + 1, (i + 1) % 2)
+        steps = 2 * per_chunk // msgs
+        direct = per_chunk // msgs
+
+        def scores(block, message, slot):
+            q = qq[pl.ds(pl.multiple_of(block * m_d, m_d), m_d)]
+            s_buf[slot] = dot_t(kv[pl.ds(message, msgs)].reshape(bk, LANES), q)
+
+        for c in range(CHUNKS):
+            if c + 1 < CHUNKS:
+                relay(phase, kv, c + 1)
+            relayed(phase, kv, c)
+            places = [c * per_chunk + i * msgs for i in range(direct)] + [chips + c * per_chunk + i * msgs for i in range(steps - direct)]
+            for t in places:
+                kvt[:, t * half:t * half + bk] = kv[t:t + msgs].reshape(bk, LANES).T
+            if c == 0:
+                scores(blocks - 1, 0, 0)
+
+            def q_block(b, _):
+                block = blocks - 1 - b
+                if c == 0:
+                    m = jnp.full((1, m_d), NEG, F32)
+                    l = jnp.zeros((1, m_d), F32)
+                    acc_a = jnp.zeros((hd_d, h_d), F32)
+                    acc_b = jnp.zeros((hd_d, h_d), F32)
                 else:
-                    scores(jnp.minimum(b + 1, blocks - 1), 0, 0)
-                s = s_buf[i % 2]
-                m_new = jnp.maximum(m, jnp.max(s, axis=0, keepdims=True))
-                p = jnp.exp2(s * c_d - m_new * c_d)
-                alphas.append(jnp.exp2((m - m_new) * c_d))
-                l = l * alphas[i] + jnp.sum(p, axis=0, keepdims=True)
-                p_buf[i % 2] = p.astype(BF16)
-                m = m_new
-                if i > 0:
-                    acc_a, acc_b = add(i - 1, acc_a, acc_b)
-            acc_a, acc_b = add(steps - 1, acc_a, acc_b)
-            m_all = jnp.maximum(m[:, :h_d], m[:, h_d:])
-            e_a = jnp.exp2((m[:, :h_d] - m_all) * c_d)
-            e_b = jnp.exp2((m[:, h_d:] - m_all) * c_d)
-            res = (acc_a * e_a + acc_b * e_b) / (l[:, :h_d] * e_a + l[:, h_d:] * e_b)
-            stacked = jnp.concatenate([res[:, j * blk:(j + 1) * blk] for j in range(parts)], axis=0)
-            o_s[pl.ds(b * per, per)] = stacked.T.astype(BF16).reshape(per, rows_q, LANES)
-
-            def home(k, _):
-                send_home(phase, k)
+                    m, l, acc_a, acc_b = m_st[block], l_st[block], acc_st[block, 0], acc_st[block, 1]
+                alphas = []
+
+                def add(i, acc_a, acc_b):
+                    keys = slice(places[i] * half, places[i] * half + bk)
+                    acc_a = acc_a * alphas[i][:, :h_d] + dot(kvt[hd_d:2 * hd_d, keys], p_buf[i % 2, :, :h_d])
+                    acc_b = acc_b * alphas[i][:, h_d:] + dot(kvt[3 * hd_d:4 * hd_d, keys], p_buf[i % 2, :, h_d:])
+                    return acc_a, acc_b
+
+                for i in range(steps):
+                    if i + 1 < steps:
+                        scores(block, places[i + 1], (i + 1) % 2)
+                    else:
+                        ahead = min(c + 1, CHUNKS - 1) - c
+                        last = b // (blocks - 1)
+                        scores(lax.rem(block + blocks - 1, blocks), (c + ahead * last) * per_chunk, 0)
+                    s = s_buf[i % 2]
+                    m_new = jnp.maximum(m, jnp.max(s, axis=0, keepdims=True))
+                    p = jnp.exp2(s * c_d - m_new * c_d)
+                    alphas.append(jnp.exp2((m - m_new) * c_d))
+                    l = l * alphas[i] + jnp.sum(p, axis=0, keepdims=True)
+                    p_buf[i % 2] = p.astype(BF16)
+                    m = m_new
+                    if i > 0:
+                        acc_a, acc_b = add(i - 1, acc_a, acc_b)
+                acc_a, acc_b = add(steps - 1, acc_a, acc_b)
+                if c + 1 < CHUNKS:
+                    m_st[block], l_st[block], acc_st[block, 0], acc_st[block, 1] = m, l, acc_a, acc_b
+                    return 0
+                m_all = jnp.maximum(m[:, :h_d], m[:, h_d:])
+                e_a = jnp.exp2((m[:, :h_d] - m_all) * c_d)
+                e_b = jnp.exp2((m[:, h_d:] - m_all) * c_d)
+                res = (acc_a * e_a + acc_b * e_b) / (l[:, :h_d] * e_a + l[:, h_d:] * e_b)
+                stacked = jnp.concatenate([res[:, j * blk:(j + 1) * blk] for j in range(parts)], axis=0)
+                o_s[pl.ds(block * per, per)] = stacked.T.astype(BF16).reshape(per, rows_q, LANES)
+                for j in range(1, per):
+                    send_home(phase, block, j)
+
+                @pl.when(block > 0)
+                def _():
+                    send_home(phase, block, 0)
                 return 0
 
-            lax.fori_loop(jnp.maximum(b * per, 1), (b + 1) * per, home, 0)
-            return 0
-
-        lax.fori_loop(0, blocks, q_block, 0)
+            lax.fori_loop(0, blocks, q_block, 0)
         o_in[phase, pair] = o_s[0]
         finish(phase, kv)
 
@@ -417,6 +463,9 @@
 
         def buf(*shape, dtype=BF16):
             return pltpu.VMEM(shape, dtype)
+
+        def sems(*shape):
+            return pltpu.SemaphoreType.DMA(shape)
 
         return pl.pallas_call(
             functools.partial(model_kernel, n, enc_heads, dec_heads),
@@ -433,8 +482,10 @@
                 buf(e_rows, d_enc), buf(e_rows, 3 * d_enc, dtype=F32), buf(e_rows, d_enc),
                 buf(d_rows, d_dec), buf(d_rows, 3 * d_dec, dtype=F32), buf(d_rows, d_dec),
                 buf(LANES, 8 * LANES),
+                buf(4, 1, m_d, dtype=F32), buf(4, 1, m_d, dtype=F32), buf(4, 2, LANES // 4, m_d // 2, dtype=F32),
                 pltpu.SemaphoreType.DMA((11,)),
-            ] + [pltpu.SemaphoreType.DMA((phases,))] * 6,
+                sems(phases), sems(phases, CHUNKS), sems(phases), sems(phases, CHUNKS), sems(phases), sems(phases), sems(phases), sems(phases),
+            ],
             compiler_params=pltpu.CompilerParams(collective_id=0, has_side_effects=True, vmem_limit_bytes=67043328),
             name='model',
         )(patches, vis_mask, enc_pos, dec_pos, b_pe.reshape(1, -1), mask_token.reshape(1, -1), w_pe,

time: 175 us -> 150 us (0.86)
  Pallas kernels: 171 us -> 144 us
    pallas_call x1, Pallas kernels: 171 us -> 144 us  [local_program(): pl.pallas_call(functools.partial(model_kernel, n, enc_heads, dec_heads),...]
where the time goes in v3:
time: 150 us; the launch traced here: 149 us
  Pallas kernels  144 us (96%)
  local copies, waits for them, and re-layouts  4.3 us (3%)
    pallas_call x1, Pallas kernels, local_program(): pl.pallas_call(functools.partial(model_kernel, n, enc_heads, dec_heads),...  144 us

profile of v3, /device:TPU:1, one launch (start us, length us, event | category | flops | bytes accessed | tf_op | source)
XLA Modules:
  0.0 148.8 jit_solution(18308270465005919090)
XLA Ops:
  0.0 1.3 reshape.19.mask_token
  1.3 1.3 reshape.18.b_pe
  2.5 144.5 %model.1 = f32[2,64,768]{2,1,0:T(8,128)} custom-call(bf16[2,64,768]{2,1,0:T(8,128)(2,1)} %patches.1, s32[2,64]{1,0:T(2,128)} %mask.1, bf16[64,1024]{1,0:T(8,128)(2,1)} %enc_pos.1, bf16[64,512]{1,0:T(8,128)(2,1)} %dec_pos.1, bf16[1,1024]{1,0:T(2,128)(2,1)} %reshape.18.b_pe, bf16[1,512]{1,0:T(2,128)(2,1)} %reshape.19.mask_token, bf16[768,1024]{1,0:T(8,128)(2,1)} %w_pe.1, ...), custom_call_target="tpu_custom_call" | custom-call | tf_op jit(solution)/shard_map/model/pallas_call | solution.py:470
  147.0 1.8 %copy.19 = f32[2,64,768]{2,1,0:T(8,128)} copy(f32[2,64,768]{2,1,0:T(8,128)} %model.1) | data formatting | bytes 786432

commit v4 on v2

--- a/solution.py
+++ b/solution.py
@@ -13,6 +13,8 @@
 MSG = 16
 LOG2E = 1.4426950408889634
 NEG = -3e38
+SIDE = 4
+CHUNKS = 4
 BF16 = jnp.bfloat16
 F32 = jnp.float32
 
@@ -45,18 +47,40 @@
     return x if shift == 0 else pltpu.roll(x, shift, 1)
 
 
+def row_of(ref):
+    rows = ref[...].astype(F32)
+    return jnp.concatenate([rows[i:i + 1] for i in range(rows.shape[0])], axis=1)
+
+
 def wait_bytes(ref, sem):
     pltpu.make_async_copy(ref, ref, sem).wait()
 
 
-def model_kernel(n, enc_heads, dec_heads, patches, mask, enc_pos, dec_pos, b_pe, mask_token,
+def model_kernel(n, enc_heads, dec_heads, mask, b_pe, mask_token, patches_h, enc_pos_h, dec_pos_h,
                  w_pe, e_qkv, e_proj, e_up, e_down, w_ed, d_qkv, d_proj, d_up, d_down, w_out, out,
-                 w_pe_s, e_qkv_s, e_proj_s, e_up_s, e_down_s, w_ed_s, d_qkv_s, d_proj_s, d_up_s, d_down_s, w_out_s,
+                 patches, enc_pos, dec_pos, w_pe_s, e_qkv_s, e_proj_s, e_up_s, e_down_s, w_ed_s, d_qkv_s, d_proj_s, d_up_s, d_down_s, w_out_s,
                  ekvm, dkvm, qm, o_s, ekv, dkv, q_in, o_in, ekvx, kvt, qq, s_buf, p_buf, hid_e, qkv_e, att_e, hid_d, qkv_d, att_d, pick_s,
-                 wsem, kv_send, kv_recv, q_send, q_recv, o_send, o_recv):
+                 m_st, l_st, acc_st, wsem, kv_send, kv_recv, f_send, f_recv, q_send, q_recv, o_send, o_recv):
     me = lax.axis_index('sp')
     groups = n // QUARTERS
     pair = me // QUARTERS
+    chips = n // 2
+    per_chunk = chips // CHUNKS
+    core = lax.rem(me, 2)
+    partner = me + 1 - 2 * core
+    at_z, at_y, at_x = me // 32, lax.rem(me // 8, SIDE), lax.rem(me // 2, SIDE)
+
+    def device_at(dz, dy, dx):
+        return (lax.rem(at_z + dz, SIDE) * SIDE + lax.rem(at_y + dy, SIDE)) * 8 + lax.rem(at_x + dx, SIDE) * 2 + core
+
+    far = {0: 0, 1: 1, 2: 2, 3: 1}
+    offsets = sorted(((dz, dy, dx) for dz in range(SIDE) for dy in range(SIDE) for dx in range(SIDE)), key=lambda o: far[o[0]] + far[o[1]] + far[o[2]])
+
+    def query_offset(block, j):
+        return 2 * lax.rem(block, 2) + j // 4, j % 4, 2 * (block // 2)
+
+    def back(d):
+        return SIDE - d
     clips, tokens, _ = patches.shape
     slots = 2 * (tokens // KEEP_DIV)
     layers = e_qkv.shape[0]
@@ -77,22 +101,28 @@
         src, dst, i = enc_loads[which]
         return load(src.at[layer], dst, i)
 
+    first_loads = [load(patches_h, patches, 11), load(enc_pos_h, enc_pos, 12), load(dec_pos_h, dec_pos, 13)]
+    for copy in first_loads:
+        copy.start()
     load_pe.start()
     enc_load(0, 0).start()
 
     barrier = pltpu.get_barrier_semaphore()
 
     def greet(i, _):
-        pl.semaphore_signal(barrier, inc=1, device_id={'sp': lax.rem(me + i, n)}, device_id_type=mesh_id)
+        pl.semaphore_signal(barrier, inc=1, device_id={'sp': lax.rem(me + 2 * i, n)}, device_id_type=mesh_id)
         return 0
 
-    lax.fori_loop(1, n, greet, 0)
+    lax.fori_loop(1, chips, greet, 0)
+    pl.semaphore_signal(barrier, inc=1, device_id={'sp': partner}, device_id_type=mesh_id)
 
     mask_f = mask[...].astype(F32)
     before = lax.broadcasted_iota(jnp.int32, (tokens, tokens), 0) < lax.broadcasted_iota(jnp.int32, (tokens, tokens), 1)
     rank = dot(mask_f.astype(BF16), before.astype(BF16))
     slot_id = lax.broadcasted_iota(jnp.int32, (slots, tokens), 0).astype(F32)
     selects, moved_x, moved_pos, occupied = [], [], [], []
+    for copy in first_loads:
+        copy.wait()
     for c in range(clips):
         select = jnp.where((rank[c:c + 1] == slot_id) & (mask_f[c:c + 1] > 0), 1.0, 0.0)
         selects.append(select)
@@ -100,40 +130,44 @@
         moved_pos.append(dot(select.astype(BF16), enc_pos[...]))
         occupied.append(jnp.sum(select, axis=1, keepdims=True))
     load_pe.wait()
-    embedded = dot(jnp.concatenate(moved_x, axis=0), w_pe_s[...]) + b_pe[...].astype(F32) + jnp.concatenate(moved_pos, axis=0)
+    embedded = dot(jnp.concatenate(moved_x, axis=0), w_pe_s[...]) + row_of(b_pe) + jnp.concatenate(moved_pos, axis=0)
     hid_e[...] = embedded.astype(BF16)
     for which in range(1, 4):
         enc_load(which, 0).start()
-    pl.semaphore_wait(barrier, n - 1)
-
-    def exchange(phase, kvm, kv):
-        def send_kv(i, _):
-            to = lax.rem(me + i, n)
+
+    def send_kv(phase, kvm, kv, order):
+        for i in order:
+            to = device_at(*offsets[i])
             pltpu.make_async_remote_copy(
-                src_ref=kvm.at[to // QUARTERS], dst_ref=kv.at[i], send_sem=kv_send.at[phase], recv_sem=kv_recv.at[phase],
+                src_ref=kvm.at[to // QUARTERS], dst_ref=kv.at[i], send_sem=kv_send.at[phase], recv_sem=kv_recv.at[phase, i // per_chunk],
                 device_id={'sp': to}, device_id_type=mesh_id).start()
-            return 0
-
-        def send_q(k, _):
-            to = lax.rem(me + QUARTERS * k, n)
+
+    def send_q(phase, order):
+        for k in order:
+            to = device_at(*query_offset(k // 8, k % 8))
             pltpu.make_async_remote_copy(
-                src_ref=qm.at[to // QUARTERS], dst_ref=q_in.at[phase, k], send_sem=q_send.at[phase], recv_sem=q_recv.at[phase],
+                src_ref=qm.at[to // QUARTERS], dst_ref=q_in.at[phase, k], send_sem=q_send.at[phase], recv_sem=q_recv.at[phase, k // 8],
                 device_id={'sp': to}, device_id_type=mesh_id).start()
-            return 0
-
-        lax.fori_loop(1, groups, send_q, 0)
-        lax.fori_loop(1, n, send_kv, 0)
-        q_in[phase, 0] = qm[pair]
-        kv[0] = kvm[pair]
-
-    def arrived(phase, kv):
-        wait_bytes(q_in.at[phase, pl.ds(1, groups - 1)], q_recv.at[phase])
-        wait_bytes(kv.at[pl.ds(1, n - 1)], kv_recv.at[phase])
-
-    def send_home(phase, k):
-        to = lax.rem(me - QUARTERS * k + n, n)
+
+    def relay(phase, kv, c):
+        first = 1 if isinstance(c, int) and c == 0 else 0
+        wait_bytes(kv.at[pl.ds(c * per_chunk + first, per_chunk - first)], kv_recv.at[phase, c])
         pltpu.make_async_remote_copy(
-            src_ref=o_s.at[k], dst_ref=o_in.at[phase, pair], send_sem=o_send.at[phase], recv_sem=o_recv.at[phase],
+            src_ref=kv.at[pl.ds(c * per_chunk, per_chunk)], dst_ref=kv.at[pl.ds(chips + c * per_chunk, per_chunk)],
+            send_sem=f_send.at[phase], recv_sem=f_recv.at[phase, c], device_id={'sp': partner}, device_id_type=mesh_id).start()
+
+    def relayed(phase, kv, c):
+        wait_bytes(kv.at[pl.ds(chips + c * per_chunk, per_chunk)], f_recv.at[phase, c])
+
+    def queries_in(phase, block):
+        first = 1 if isinstance(block, int) and block == 0 else 0
+        wait_bytes(q_in.at[phase, pl.ds(8 * block + first, 8 - first)], q_recv.at[phase, block])
+
+    def send_home(phase, block, j):
+        dz, dy, dx = query_offset(block, j)
+        to = device_at(back(dz), back(dy), back(dx))
+        pltpu.make_async_remote_copy(
+            src_ref=o_s.at[8 * block + j], dst_ref=o_in.at[phase, pair], send_sem=o_send.at[phase], recv_sem=o_recv.at[phase],
             device_id={'sp': to}, device_id_type=mesh_id).start()
 
     def finish(phase, kv):
@@ -141,7 +175,8 @@
         wait_bytes(o_in.at[phase, rest], o_recv.at[phase])
         wait_bytes(o_s.at[rest], o_send.at[phase])
         wait_bytes(qm.at[rest], q_send.at[phase])
-        wait_bytes(kv.at[pl.ds(1, n - 1)], kv_send.at[phase])
+        wait_bytes(kv.at[pl.ds(1, chips - 1)], kv_send.at[phase])
+        wait_bytes(kv.at[pl.ds(0, chips)], f_send.at[phase])
 
     hd_e = d_enc // enc_heads
     lane_e = lane_of((slots, LANES))
@@ -153,27 +188,40 @@
     def enc_layer(layer, _):
         normed = layer_norm(hid_e[...])
         enc_load(0, layer).wait()
-        for t in range(0, 3 * d_enc, 1024):
+        for t in range(d_enc, 3 * d_enc, 1024):
             qkv_e[:, t:t + 1024] = dot_t(normed, e_qkv_s[t:t + 1024])
-
-        @pl.when(layer + 1 < layers)
-        def _():
-            enc_load(0, layer + 1).start()
 
         for c in range(clips):
             rows = slice(c * slots, (c + 1) * slots)
             for h in range(enc_heads):
                 tile = (h * hd_e) // LANES * LANES
                 off = h * hd_e - tile
-                q_t = roll(qkv_e[rows, tile:tile + LANES], -off)
                 k_t = roll(qkv_e[rows, d_enc + tile:d_enc + tile + LANES], -off)
                 v_t = roll(qkv_e[rows, 2 * d_enc + tile:2 * d_enc + tile + LANES], hd_e - off)
-                qm[c * enc_heads + h] = jnp.where(lane_e < hd_e, q_t, 0.0).astype(BF16)
                 kv_t = jnp.where(lane_e < hd_e, k_t, v_t)
                 ekvm[c * enc_heads + h] = jnp.where(occupied[c] > 0, kv_t, jnp.inf).astype(BF16)
 
         kv = ekv.at[layer]
-        exchange(layer, ekvm, kv)
+
+        @pl.when(layer == 0)
+        def _():
+            pl.semaphore_wait(barrier, chips)
+
+        send_kv(layer, ekvm, kv, range(chips - 1, 0, -1))
+        qkv_e[:, :d_enc] = dot_t(normed, e_qkv_s[:d_enc])
+        for c in range(clips):
+            rows = slice(c * slots, (c + 1) * slots)
+            for h in range(enc_heads):
+                tile = (h * hd_e) // LANES * LANES
+                q_t = roll(qkv_e[rows, tile:tile + LANES], tile - h * hd_e)
+                qm[c * enc_heads + h] = jnp.where(lane_e < hd_e, q_t, 0.0).astype(BF16)
+        send_q(layer, range(groups - 1, 0, -1))
+        q_in[layer, 0] = qm[pair]
+        kv[0] = ekvm[pair]
+
+        @pl.when(layer + 1 < layers)
+        def _():
+            enc_load(0, layer + 1).start()
 
         @pl.when(layer == 0)
         def _():
@@ -182,7 +230,12 @@
                 copy.start()
             load_out.start()
 
-        arrived(layer, kv)
+        for c in (2, 1, 0, 3):
+            relay(layer, kv, c)
+        for block in range(4):
+            queries_in(layer, block)
+        for c in (2, 1, 0, 3):
+            relayed(layer, kv, c)
         for t in range(0, n, 32):
             block = kv[t:t + 32].reshape(32 * slots, LANES)
             bad = block == jnp.inf
@@ -221,12 +274,9 @@
         both = jnp.concatenate([jnp.where(odd, zero, res), jnp.where(odd, res, zero)], axis=0)
         o_s[...] = both.T.astype(BF16).reshape(groups, slots, LANES)
 
-        def home(k, _):
-            send_home(layer, k)
-            return 0
-
         o_in[layer, pair] = o_s[0]
-        lax.fori_loop(1, groups, home, 0)
+        for k in range(groups - 1, 0, -1):
+            send_home(layer, k // 8, k % 8)
         finish(layer, kv)
 
         for c in range(clips):
@@ -264,7 +314,7 @@
     for c in range(clips):
         placed = lax.dot_general(selects[c].astype(BF16), z[c * slots:(c + 1) * slots], (((0,), (0,)), ((), ())), preferred_element_type=F32)
         seen = jnp.max(selects[c].T, axis=1, keepdims=True)
-        token = jnp.where(seen > 0, placed, mask_token[...].astype(F32))
+        token = jnp.where(seen > 0, placed, row_of(mask_token))
         hid_d[c * tokens:(c + 1) * tokens] = (token + dec_pos[...].astype(F32)).astype(BF16)
 
     hd_d = d_dec // dec_heads
@@ -291,7 +341,8 @@
     def dec_layer(layer, _):
         phase = layers + layer
         normed = layer_norm(hid_d[...])
-        qkv_d[...] = dot_t(normed, d_qkv_s[layer])
+        kv = dkv.at[layer]
+        qkv_d[:, d_dec:] = dot_t(normed, d_qkv_s[layer, d_dec:])
         for c in range(clips):
             base = c * tokens
             for h in range(dec_heads):
@@ -305,50 +356,56 @@
                 k_hi, v_hi = roll(qkv_d[hi, kc], 2 * hd_d - off), roll(qkv_d[hi, vc], 3 * hd_d - off)
                 dkvm[c * dec_heads + h] = jnp.where(
                     lane_k < 2 * hd_d, jnp.where(lane_k < hd_d, k_lo, v_lo), jnp.where(lane_k < 3 * hd_d, k_hi, v_hi)).astype(BF16)
+        send_kv(phase, dkvm, kv, range(1, per_chunk))
+        qkv_d[:, :d_dec] = dot_t(normed, d_qkv_s[layer, :d_dec])
+        for c in range(clips):
+            base = c * tokens
+            for h in range(dec_heads):
+                tile = (h * hd_d) // LANES * LANES
+                off = h * hd_d - tile
                 packed = None
                 for j in range(parts):
                     moved = roll(qkv_d[base + j * rows_q:base + (j + 1) * rows_q, tile:tile + LANES], hd_d * j - off)
                     packed = moved if packed is None else jnp.where(lane_q >= hd_d * j, moved, packed)
                 qm[c * dec_heads + h] = packed.astype(BF16)
-        kv = dkv.at[layer]
-        exchange(phase, dkvm, kv)
-        arrived(phase, kv)
-
-        spread = dot(q_in[phase].reshape(q_rows, LANES), pick_s[...])
-        for b in range(q_rows // blk):
-            for t in range(2 * parts):
-                qq[b * m_d + t * blk:b * m_d + (t + 1) * blk] = spread[b * blk:(b + 1) * blk, t * LANES:(t + 1) * LANES].astype(BF16)
-        for t in range(0, n, 16):
-            kvt[:, t * half:(t + 16) * half] = kv[t:t + 16].reshape(16 * half, LANES).T
-
-        steps = n_d // bk
+        send_q(phase, range(1, groups))
+        send_kv(phase, dkvm, kv, range(per_chunk, chips))
+        q_in[phase, 0] = qm[pair]
+        kv[0] = dkvm[pair]
+
         msgs = bk // half
         blocks = q_rows // blk
 
-        def scores(b, i, slot):
-            q = qq[pl.ds(pl.multiple_of(b * m_d, m_d), m_d)]
-            s_buf[slot] = dot_t(kv[i * msgs:(i + 1) * msgs].reshape(bk, LANES), q)
-
-        scores(0, 0, 0)
-
-        def q_block(b, _):
-            m = jnp.full((1, m_d), NEG, F32)
-            l = jnp.zeros((1, m_d), F32)
-            acc_a = jnp.zeros((hd_d, h_d), F32)
-            acc_b = jnp.zeros((hd_d, h_d), F32)
+        def spread(block):
+            queries_in(phase, block)
+            wide = dot(q_in[phase, pl.ds(8 * block, 8)].reshape(blk, LANES), pick_s[...])
+            for t in range(2 * parts):
+                qq[pl.ds(pl.multiple_of(block * m_d + t * blk, blk), blk)] = wide[:, t * LANES:(t + 1) * LANES].astype(BF16)
+
+        def transpose(places):
+            for t in places:
+                kvt[:, t * half:t * half + bk] = kv[t:t + msgs].reshape(bk, LANES).T
+
+        def scores(block, message, slot):
+            q = qq[pl.ds(pl.multiple_of(block * m_d, m_d), m_d)]
+            s_buf[slot] = dot_t(kv[pl.ds(message, msgs)].reshape(bk, LANES), q)
+
+        def attend(block, places, state, next_block, next_message):
+            m, l, acc_a, acc_b = state
             alphas = []
+            steps = len(places)
 
             def add(i, acc_a, acc_b):
-                keys = slice(i * bk, (i + 1) * bk)
+                keys = slice(places[i] * half, places[i] * half + bk)
                 acc_a = acc_a * alphas[i][:, :h_d] + dot(kvt[hd_d:2 * hd_d, keys], p_buf[i % 2, :, :h_d])
                 acc_b = acc_b * alphas[i][:, h_d:] + dot(kvt[3 * hd_d:4 * hd_d, keys], p_buf[i % 2, :, h_d:])
                 return acc_a, acc_b
 
             for i in range(steps):
                 if i + 1 < steps:
-                    scores(b, i + 1, (i + 1) % 2)
+                    scores(block, places[i + 1], (i + 1) % 2)
                 else:
-                    scores(jnp.minimum(b + 1, blocks - 1), 0, 0)
+                    scores(next_block, next_message, 0)
                 s = s_buf[i % 2]
                 m_new = jnp.maximum(m, jnp.max(s, axis=0, keepdims=True))
                 p = jnp.exp2(s * c_d - m_new * c_d)
@@ -359,21 +416,58 @@
                 if i > 0:
                     acc_a, acc_b = add(i - 1, acc_a, acc_b)
             acc_a, acc_b = add(steps - 1, acc_a, acc_b)
+            return m, l, acc_a, acc_b
+
+        near = [i for i in range(0, per_chunk, msgs)]
+        near = near + [chips + i for i in near]
+        rest = [i for i in range(per_chunk, chips, msgs)]
+        rest = rest + [chips + i for i in rest]
+
+        relay(phase, kv, 0)
+        spread(0)
+        spread(1)
+        relayed(phase, kv, 0)
+        transpose(near)
+        scores(0, near[0], 0)
+
+        def near_block(b, _):
+            @pl.when(b > 0)
+            def _():
+                relay(phase, kv, b)
+
+            @pl.when(b + 2 < blocks)
+            def _():
+                spread(b + 2)
+
+            fresh = (jnp.full((1, m_d), NEG, F32), jnp.zeros((1, m_d), F32), jnp.zeros((hd_d, h_d), F32), jnp.zeros((hd_d, h_d), F32))
+            state = attend(b, near, fresh, jnp.minimum(b + 1, blocks - 1), near[0] + (b // (blocks - 1)) * (rest[0] - near[0]))
+            m_st[b], l_st[b], acc_st[b, 0], acc_st[b, 1] = state
+            return 0
+
+        lax.fori_loop(0, blocks, near_block, 0)
+        for c in range(1, CHUNKS):
+            relayed(phase, kv, c)
+        transpose(rest)
+
+        def rest_block(b, _):
+            block = blocks - 1 - b
+            state = (m_st[block], l_st[block], acc_st[block, 0], acc_st[block, 1])
+            m, l, acc_a, acc_b = attend(block, rest, state, lax.rem(block + blocks - 1, blocks), rest[0])
             m_all = jnp.maximum(m[:, :h_d], m[:, h_d:])
             e_a = jnp.exp2((m[:, :h_d] - m_all) * c_d)
             e_b = jnp.exp2((m[:, h_d:] - m_all) * c_d)
             res = (acc_a * e_a + acc_b * e_b) / (l[:, :h_d] * e_a + l[:, h_d:] * e_b)
             stacked = jnp.concatenate([res[:, j * blk:(j + 1) * blk] for j in range(parts)], axis=0)
-            o_s[pl.ds(b * per, per)] = stacked.T.astype(BF16).reshape(per, rows_q, LANES)
-
-            def home(k, _):
-                send_home(phase, k)
-                return 0
-
-            lax.fori_loop(jnp.maximum(b * per, 1), (b + 1) * per, home, 0)
+            o_s[pl.ds(block * per, per)] = stacked.T.astype(BF16).reshape(per, rows_q, LANES)
+            for j in range(1, per):
+                send_home(phase, block, j)
+
+            @pl.when(block > 0)
+            def _():
+                send_home(phase, block, 0)
             return 0
 
-        lax.fori_loop(0, blocks, q_block, 0)
+        lax.fori_loop(0, blocks, rest_block, 0)
         o_in[phase, pair] = o_s[0]
         finish(phase, kv)
 
@@ -418,12 +512,16 @@
         def buf(*shape, dtype=BF16):
             return pltpu.VMEM(shape, dtype)
 
+        def sems(*shape):
+            return pltpu.SemaphoreType.DMA(shape)
+
         return pl.pallas_call(
             functools.partial(model_kernel, n, enc_heads, dec_heads),
             out_shape=jax.ShapeDtypeStruct((clips, tokens, w_out.shape[1]), F32),
-            in_specs=[vmem] * 6 + [hbm] * 11,
+            in_specs=[vmem] * 3 + [hbm] * 14,
             out_specs=vmem,
             scratch_shapes=[
+                buf(clips, tokens, width), buf(tokens, d_enc), buf(tokens, d_dec),
                 buf(width, d_enc), buf(3 * d_enc, d_enc), buf(d_enc, d_enc), buf(d_enc, f_enc), buf(f_enc, d_enc), buf(d_enc, d_dec),
                 buf(layers, 3 * d_dec, d_dec), buf(layers, d_dec, d_dec), buf(layers, d_dec, f_dec), buf(layers, f_dec, d_dec), buf(d_dec, w_out.shape[1]),
                 buf(groups, slots, LANES), buf(groups, half, LANES), buf(groups, MSG, LANES), buf(groups, MSG, LANES),
@@ -433,11 +531,13 @@
                 buf(e_rows, d_enc), buf(e_rows, 3 * d_enc, dtype=F32), buf(e_rows, d_enc),
                 buf(d_rows, d_dec), buf(d_rows, 3 * d_dec, dtype=F32), buf(d_rows, d_dec),
                 buf(LANES, 8 * LANES),
-                pltpu.SemaphoreType.DMA((11,)),
-            ] + [pltpu.SemaphoreType.DMA((phases,))] * 6,
+                buf(4, 1, m_d, dtype=F32), buf(4, 1, m_d, dtype=F32), buf(4, 2, LANES // 4, m_d // 2, dtype=F32),
+                pltpu.SemaphoreType.DMA((14,)),
+                sems(phases), sems(phases, CHUNKS), sems(phases), sems(phases, CHUNKS), sems(phases), sems(phases, 4), sems(phases), sems(phases),
+            ],
             compiler_params=pltpu.CompilerParams(collective_id=0, has_side_effects=True, vmem_limit_bytes=67043328),
             name='model',
-        )(patches, vis_mask, enc_pos, dec_pos, b_pe.reshape(1, -1), mask_token.reshape(1, -1), w_pe,
+        )(vis_mask, b_pe.reshape(-1, LANES), mask_token.reshape(-1, LANES), patches, enc_pos, dec_pos, w_pe,
           enc_qkv.transpose(0, 2, 3, 4, 1).reshape(layers, 3 * d_enc, d_enc), enc_proj.reshape(layers, d_enc, d_enc), enc_up, enc_down, w_ed,
           dec_qkv.transpose(0, 2, 3, 4, 1).reshape(layers, 3 * d_dec, d_dec), dec_proj.reshape(layers, d_dec, d_dec), dec_up, dec_down, w_out)
 

time: 175 us -> 143 us (0.82)
  Pallas kernels: 171 us -> 141 us
  local copies, waits for them, and re-layouts: 4.3 us -> 1.77 us
    pallas_call x1, Pallas kernels: 171 us -> 141 us  [local_program(): pl.pallas_call(functools.partial(model_kernel, n, enc_heads, dec_heads),...]
    reshape x2 -> x0, local copies, waits for them, and re-layouts: 2.53 us -> none  [the longest x1 1.28 us: local_program(): b_pe.reshape(1, -1)]
where the time goes in v4:
time: 143 us
  Pallas kernels  141 us (99%)
  local copies, waits for them, and re-layouts  1.77 us (1%)
    pallas_call x1, Pallas kernels, local_program(): pl.pallas_call(functools.partial(model_kernel, n, enc_heads, dec_heads),...  141 us

profile of v4, /device:TPU:1, one launch (start us, length us, event | category | flops | bytes accessed | tf_op | source)
XLA Modules:
  0.0 142.7 jit_solution(414385579768797228)
XLA Ops:
  0.0 140.9 %model.1 = f32[2,64,768]{2,1,0:T(8,128)} custom-call(s32[2,64]{1,0:T(2,128)} %mask.1, bf16[8,128]{1,0:T(8,128)(2,1)} %bitcast.14, bf16[4,128]{1,0:T(4,128)(2,1)} %bitcast.15, bf16[2,64,768]{2,1,0:T(8,128)(2,1)} %patches_h.1, bf16[64,1024]{1,0:T(8,128)(2,1)} %enc_pos_h.1, bf16[64,512]{1,0:T(8,128)(2,1)} %dec_pos_h.1, bf16[768,1024]{1,0:T(8,128)(2,1)} %w_pe.1, ...), custom_call_target="tpu_custom_call" | custom-call | tf_op jit(solution)/shard_map/model/pallas_call | solution.py:518
  140.9 1.8 %copy.19 = f32[2,64,768]{2,1,0:T(8,128)} copy(f32[2,64,768]{2,1,0:T(8,128)} %model.1) | data formatting | bytes 786432

commit v5 on v4

--- a/solution.py
+++ b/solution.py
@@ -420,8 +420,6 @@
 
         near = [i for i in range(0, per_chunk, msgs)]
         near = near + [chips + i for i in near]
-        rest = [i for i in range(per_chunk, chips, msgs)]
-        rest = rest + [chips + i for i in rest]
 
         relay(phase, kv, 0)
         spread(0)
@@ -440,34 +438,46 @@
                 spread(b + 2)
 
             fresh = (jnp.full((1, m_d), NEG, F32), jnp.zeros((1, m_d), F32), jnp.zeros((hd_d, h_d), F32), jnp.zeros((hd_d, h_d), F32))
-            state = attend(b, near, fresh, jnp.minimum(b + 1, blocks - 1), near[0] + (b // (blocks - 1)) * (rest[0] - near[0]))
+            state = attend(b, near, fresh, jnp.minimum(b + 1, blocks - 1), b // (blocks - 1) * per_chunk)
             m_st[b], l_st[b], acc_st[b, 0], acc_st[b, 1] = state
             return 0
 
         lax.fori_loop(0, blocks, near_block, 0)
         for c in range(1, CHUNKS):
+            places = [c * per_chunk + i for i in near]
             relayed(phase, kv, c)
-        transpose(rest)
-
-        def rest_block(b, _):
-            block = blocks - 1 - b
-            state = (m_st[block], l_st[block], acc_st[block, 0], acc_st[block, 1])
-            m, l, acc_a, acc_b = attend(block, rest, state, lax.rem(block + blocks - 1, blocks), rest[0])
-            m_all = jnp.maximum(m[:, :h_d], m[:, h_d:])
-            e_a = jnp.exp2((m[:, :h_d] - m_all) * c_d)
-            e_b = jnp.exp2((m[:, h_d:] - m_all) * c_d)
-            res = (acc_a * e_a + acc_b * e_b) / (l[:, :h_d] * e_a + l[:, h_d:] * e_b)
-            stacked = jnp.concatenate([res[:, j * blk:(j + 1) * blk] for j in range(parts)], axis=0)
-            o_s[pl.ds(block * per, per)] = stacked.T.astype(BF16).reshape(per, rows_q, LANES)
-            for j in range(1, per):
-                send_home(phase, block, j)
-
-            @pl.when(block > 0)
-            def _():
-                send_home(phase, block, 0)
-            return 0
-
-        lax.fori_loop(0, blocks, rest_block, 0)
+            transpose(places)
+
+            def rest_block(b, _):
+                block = blocks - 1 - b if c % 2 else b
+                if c + 1 == CHUNKS:
+                    next_block = jnp.maximum(block - 1, 0)
+                elif c % 2:
+                    next_block = jnp.maximum(block - 1, 0)
+                else:
+                    next_block = jnp.minimum(block + 1, blocks - 1)
+                ahead = 1 if c + 1 < CHUNKS else 0
+                state = (m_st[block], l_st[block], acc_st[block, 0], acc_st[block, 1])
+                state = attend(block, places, state, next_block, (c + b // (blocks - 1) * ahead) * per_chunk)
+                m, l, acc_a, acc_b = state
+                if c + 1 < CHUNKS:
+                    m_st[block], l_st[block], acc_st[block, 0], acc_st[block, 1] = state
+                    return 0
+                m_all = jnp.maximum(m[:, :h_d], m[:, h_d:])
+                e_a = jnp.exp2((m[:, :h_d] - m_all) * c_d)
+                e_b = jnp.exp2((m[:, h_d:] - m_all) * c_d)
+                res = (acc_a * e_a + acc_b * e_b) / (l[:, :h_d] * e_a + l[:, h_d:] * e_b)
+                stacked = jnp.concatenate([res[:, j * blk:(j + 1) * blk] for j in range(parts)], axis=0)
+                o_s[pl.ds(block * per, per)] = stacked.T.astype(BF16).reshape(per, rows_q, LANES)
+                for j in range(1, per):
+                    send_home(phase, block, j)
+
+                @pl.when(block > 0)
+                def _():
+                    send_home(phase, block, 0)
+                return 0
+
+            lax.fori_loop(0, blocks, rest_block, 0)
         o_in[phase, pair] = o_s[0]
         finish(phase, kv)
 

time: 143 us -> 141 us (0.986)
  Pallas kernels: 141 us -> 139 us
    pallas_call x1, Pallas kernels: 141 us -> 139 us  [local_program(): pl.pallas_call(functools.partial(model_kernel, n, enc_heads, dec_heads),...]
where the time goes in v5:
time: 141 us
  Pallas kernels  139 us (99%)
  local copies, waits for them, and re-layouts  1.77 us (1%)
    pallas_call x1, Pallas kernels, local_program(): pl.pallas_call(functools.partial(model_kernel, n, enc_heads, dec_heads),...  139 us

profile of v5, /device:TPU:1, one launch (start us, length us, event | category | flops | bytes accessed | tf_op | source)
XLA Modules:
  0.0 140.6 jit_solution(13137880747663653903)
XLA Ops:
  0.0 138.8 %model.1 = f32[2,64,768]{2,1,0:T(8,128)} custom-call(s32[2,64]{1,0:T(2,128)} %mask.1, bf16[8,128]{1,0:T(8,128)(2,1)} %bitcast.14, bf16[4,128]{1,0:T(4,128)(2,1)} %bitcast.15, bf16[2,64,768]{2,1,0:T(8,128)(2,1)} %patches_h.1, bf16[64,1024]{1,0:T(8,128)(2,1)} %enc_pos_h.1, bf16[64,512]{1,0:T(8,128)(2,1)} %dec_pos_h.1, bf16[768,1024]{1,0:T(8,128)(2,1)} %w_pe.1, ...), custom_call_target="tpu_custom_call" | custom-call | tf_op jit(solution)/shard_map/model/pallas_call | solution.py:528
  138.8 1.8 %copy.19 = f32[2,64,768]{2,1,0:T(8,128)} copy(f32[2,64,768]{2,1,0:T(8,128)} %model.1) | data formatting | bytes 786432

commit v6 on v5

--- a/solution.py
+++ b/solution.py
@@ -59,7 +59,7 @@
 def model_kernel(n, enc_heads, dec_heads, mask, b_pe, mask_token, patches_h, enc_pos_h, dec_pos_h,
                  w_pe, e_qkv, e_proj, e_up, e_down, w_ed, d_qkv, d_proj, d_up, d_down, w_out, out,
                  patches, enc_pos, dec_pos, w_pe_s, e_qkv_s, e_proj_s, e_up_s, e_down_s, w_ed_s, d_qkv_s, d_proj_s, d_up_s, d_down_s, w_out_s,
-                 ekvm, dkvm, qm, o_s, ekv, dkv, q_in, o_in, ekvx, kvt, qq, s_buf, p_buf, hid_e, qkv_e, att_e, hid_d, qkv_d, att_d, pick_s,
+                 ekvm, dkvm, eqm, dqm, o_s, ekv, dkv, eq_in, dq_in, o_in, ekvx, kvt, qq, s_buf, p_buf, hid_e, qkv_e, att_e, hid_d, qkv_d, att_d, pick_s,
                  m_st, l_st, acc_st, wsem, kv_send, kv_recv, f_send, f_recv, q_send, q_recv, o_send, o_recv):
     me = lax.axis_index('sp')
     groups = n // QUARTERS
@@ -142,11 +142,11 @@
                 src_ref=kvm.at[to // QUARTERS], dst_ref=kv.at[i], send_sem=kv_send.at[phase], recv_sem=kv_recv.at[phase, i // per_chunk],
                 device_id={'sp': to}, device_id_type=mesh_id).start()
 
-    def send_q(phase, order):
+    def send_q(phase, qm, q_in, order):
         for k in order:
             to = device_at(*query_offset(k // 8, k % 8))
             pltpu.make_async_remote_copy(
-                src_ref=qm.at[to // QUARTERS], dst_ref=q_in.at[phase, k], send_sem=q_send.at[phase], recv_sem=q_recv.at[phase, k // 8],
+                src_ref=qm.at[to // QUARTERS], dst_ref=q_in.at[k], send_sem=q_send.at[phase], recv_sem=q_recv.at[phase, k // 8],
                 device_id={'sp': to}, device_id_type=mesh_id).start()
 
     def relay(phase, kv, c):
@@ -159,9 +159,9 @@
     def relayed(phase, kv, c):
         wait_bytes(kv.at[pl.ds(chips + c * per_chunk, per_chunk)], f_recv.at[phase, c])
 
-    def queries_in(phase, block):
+    def queries_in(phase, q_in, block):
         first = 1 if isinstance(block, int) and block == 0 else 0
-        wait_bytes(q_in.at[phase, pl.ds(8 * block + first, 8 - first)], q_recv.at[phase, block])
+        wait_bytes(q_in.at[pl.ds(8 * block + first, 8 - first)], q_recv.at[phase, block])
 
     def send_home(phase, block, j):
         dz, dy, dx = query_offset(block, j)
@@ -170,7 +170,7 @@
             src_ref=o_s.at[8 * block + j], dst_ref=o_in.at[phase, pair], send_sem=o_send.at[phase], recv_sem=o_recv.at[phase],
             device_id={'sp': to}, device_id_type=mesh_id).start()
 
-    def finish(phase, kv):
+    def finish(phase, kv, qm):
         rest = pl.ds(1, groups - 1)
         wait_bytes(o_in.at[phase, rest], o_recv.at[phase])
         wait_bytes(o_s.at[rest], o_send.at[phase])
@@ -214,9 +214,11 @@
             for h in range(enc_heads):
                 tile = (h * hd_e) // LANES * LANES
                 q_t = roll(qkv_e[rows, tile:tile + LANES], tile - h * hd_e)
-                qm[c * enc_heads + h] = jnp.where(lane_e < hd_e, q_t, 0.0).astype(BF16)
-        send_q(layer, range(groups - 1, 0, -1))
-        q_in[layer, 0] = qm[pair]
+                low = slots // 2
+                eqm[c * enc_heads + h] = jnp.where(lane_of((low, LANES)) < hd_e, q_t[:low], roll(q_t[low:], hd_e)).astype(BF16)
+        eq = eq_in.at[layer]
+        send_q(layer, eqm, eq, range(groups - 1, 0, -1))
+        eq[0] = eqm[pair]
         kv[0] = ekvm[pair]
 
         @pl.when(layer + 1 < layers)
@@ -233,7 +235,7 @@
         for c in (2, 1, 0, 3):
             relay(layer, kv, c)
         for block in range(4):
-            queries_in(layer, block)
+            queries_in(layer, eq, block)
         for c in (2, 1, 0, 3):
             relayed(layer, kv, c)
         for t in range(0, n, 32):
@@ -244,7 +246,9 @@
             ekvx[r, :LANES] = clean
             ekvx[r, LANES:] = jnp.where(bad & (lane_of(block.shape) == 0), jnp.full_like(block, NEG), jnp.zeros_like(block))
             kvt[:, r] = clean.T
-        q = q_in[layer].reshape(m_e, LANES)
+        q = eq[...].astype(F32).reshape(m_e // 2, LANES)
+        own = lane_of(q.shape) < hd_e
+        q = jnp.concatenate([jnp.where(own, q, 0.0), jnp.where(own, roll(q, hd_e), 0.0)], axis=0).astype(BF16)
         q = jnp.concatenate([q, (lane_of(q.shape) == 0).astype(BF16)], axis=1)
         steps = n_e // bk
         m = jnp.full((1, m_e), NEG, F32)
@@ -272,12 +276,15 @@
         odd = lax.rem(pair, 2) == 1
         zero = jnp.zeros_like(res)
         both = jnp.concatenate([jnp.where(odd, zero, res), jnp.where(odd, res, zero)], axis=0)
-        o_s[...] = both.T.astype(BF16).reshape(groups, slots, LANES)
+        both = both.T
+        low = slots // 2
+        o_s[...] = jnp.concatenate([
+            both[:m_e // 2].reshape(groups, low, LANES), both[m_e // 2:].reshape(groups, low, LANES)], axis=1).astype(BF16)
 
         o_in[layer, pair] = o_s[0]
         for k in range(groups - 1, 0, -1):
             send_home(layer, k // 8, k % 8)
-        finish(layer, kv)
+        finish(layer, kv, eqm)
 
         for c in range(clips):
             for g in range(enc_heads // 2):
@@ -367,18 +374,19 @@
                 for j in range(parts):
                     moved = roll(qkv_d[base + j * rows_q:base + (j + 1) * rows_q, tile:tile + LANES], hd_d * j - off)
                     packed = moved if packed is None else jnp.where(lane_q >= hd_d * j, moved, packed)
-                qm[c * dec_heads + h] = packed.astype(BF16)
-        send_q(phase, range(1, groups))
+                dqm[c * dec_heads + h] = packed.astype(BF16)
+        dq = dq_in.at[layer]
+        send_q(phase, dqm, dq, range(1, groups))
         send_kv(phase, dkvm, kv, range(per_chunk, chips))
-        q_in[phase, 0] = qm[pair]
+        dq[0] = dqm[pair]
         kv[0] = dkvm[pair]
 
         msgs = bk // half
         blocks = q_rows // blk
 
         def spread(block):
-            queries_in(phase, block)
-            wide = dot(q_in[phase, pl.ds(8 * block, 8)].reshape(blk, LANES), pick_s[...])
+            queries_in(phase, dq, block)
+            wide = dot(dq[pl.ds(8 * block, 8)].reshape(blk, LANES), pick_s[...])
             for t in range(2 * parts):
                 qq[pl.ds(pl.multiple_of(block * m_d + t * blk, blk), blk)] = wide[:, t * LANES:(t + 1) * LANES].astype(BF16)
 
@@ -479,7 +487,7 @@
 
             lax.fori_loop(0, blocks, rest_block, 0)
         o_in[phase, pair] = o_s[0]
-        finish(phase, kv)
+        finish(phase, kv, dqm)
 
         for c in range(clips):
             for g in range(dec_heads // parts):
@@ -534,8 +542,8 @@
                 buf(clips, tokens, width), buf(tokens, d_enc), buf(tokens, d_dec),
                 buf(width, d_enc), buf(3 * d_enc, d_enc), buf(d_enc, d_enc), buf(d_enc, f_enc), buf(f_enc, d_enc), buf(d_enc, d_dec),
                 buf(layers, 3 * d_dec, d_dec), buf(layers, d_dec, d_dec), buf(layers, d_dec, f_dec), buf(layers, f_dec, d_dec), buf(d_dec, w_out.shape[1]),
-                buf(groups, slots, LANES), buf(groups, half, LANES), buf(groups, MSG, LANES), buf(groups, MSG, LANES),
-                buf(layers, n, slots, LANES), buf(layers, n, half, LANES), buf(phases, groups, MSG, LANES), buf(phases, groups, MSG, LANES),
+                buf(groups, slots, LANES), buf(groups, half, LANES), buf(groups, slots // 2, LANES), buf(groups, MSG, LANES), buf(groups, MSG, LANES),
+                buf(layers, n, slots, LANES), buf(layers, n, half, LANES), buf(layers, groups, slots // 2, LANES), buf(layers, groups, MSG, LANES), buf(phases, groups, MSG, LANES),
                 buf(n * slots, 2 * LANES), buf(LANES, n * half), buf(groups * MSG * 8, LANES),
                 buf(2, bk, m_d, dtype=F32), buf(2, bk, m_d),
                 buf(e_rows, d_enc), buf(e_rows, 3 * d_enc, dtype=F32), buf(e_rows, d_enc),

time: 141 us -> 141 us (level)
  no operation moved by 1% of the time
where the time goes in v6:
time: 141 us
  Pallas kernels  139 us (99%)
  local copies, waits for them, and re-layouts  1.77 us (1%)
    pallas_call x1, Pallas kernels, local_program(): pl.pallas_call(functools.partial(model_kernel, n, enc_heads, dec_heads),...  139 us

profile of v6, /device:TPU:1, one launch (start us, length us, event | category | flops | bytes accessed | tf_op | source)
XLA Modules:
  0.0 141.1 jit_solution(14038792332659452533)
XLA Ops:
  0.0 139.3 %model.1 = f32[2,64,768]{2,1,0:T(8,128)} custom-call(s32[2,64]{1,0:T(2,128)} %mask.1, bf16[8,128]{1,0:T(8,128)(2,1)} %bitcast.14, bf16[4,128]{1,0:T(4,128)(2,1)} %bitcast.15, bf16[2,64,768]{2,1,0:T(8,128)(2,1)} %patches_h.1, bf16[64,1024]{1,0:T(8,128)(2,1)} %enc_pos_h.1, bf16[64,512]{1,0:T(8,128)(2,1)} %dec_pos_h.1, bf16[768,1024]{1,0:T(8,128)(2,1)} %w_pe.1, ...), custom_call_target="tpu_custom_call" | custom-call | tf_op jit(solution)/shard_map/model/pallas_call | solution.py:536
  139.4 1.8 %copy.19 = f32[2,64,768]{2,1,0:T(8,128)} copy(f32[2,64,768]{2,1,0:T(8,128)} %model.1) | data formatting | bytes 786432
